TPU v7x, 32 devices: a whole 2x2x4 slice. The times are simulated.
32 devices in a mesh: sp: 16 (over z, y, core), dp: 2 (over x).
Axes of the slice: x: 2, y: 2, z: 4, core: 2. Of those that a mesh axis runs over, the one named last changes fastest.
Arguments:
- query_proj: bfloat16 [4096, 8192], P(('dp', 'sp')), parts along dimension 0, may hold values from -64 to 64
- key_projection: bfloat16 [4096, 1024], P(('dp', 'sp')), parts along dimension 0, may hold values from -64 to 64
- value_projection: bfloat16 [4096, 1024], P(('dp', 'sp')), parts along dimension 0, may hold values from -12 to 12
- query_gain: float32 [128], replicated, may hold values from 1 to 5
- key_norm_gain: float32 [128], replicated, may hold values from 1 to 5
- positions: int32 [4096], P(('dp', 'sp')), parts along dimension 0, may hold values from 0 to 5118, as said below
- doc_start: int32 [4096], P(('dp', 'sp')), parts along dimension 0, may hold values from 0 to 2047, as said below
Outputs:
- attention: bfloat16 [4096, 8192], P(('dp', 'sp')), parts along dimension 0
There are 2 independent parts, one for each index of `dp`. A program takes and returns all parts, laid end to end along the dimension named above; an argument that names none is the same for every part. Nothing has to cross between parts.
Inputs may be any that keep to these rules, and one draw needn't show every extreme that they name: doc_start[i] is the index of the first token of token i's document: it never falls, doc_start[i] <= i < doc_start[i] + 1024, some document has exactly 1024 tokens, and every document but the last has 128 tokens or more. `positions`: within one document the position rises by one from each token to the next.
All inputs are finite; a program needn't handle non-finite values.
Results may differ from a plain program's by a relative error of at most 0.0039.
The roundings to bfloat16 on the way count: a program that leaves them out, or rounds other values in their place, can miss the bound.
Values may be sent and summed in bfloat16 or wider, within the bound.
A program may use at most 64 MiB of HBM per device.

v0:
```python
import functools
import math

import jax
import jax.numpy as jnp
import numpy as np
from jax import lax
from jax.experimental import pallas as pl
from jax.experimental.pallas import tpu as pltpu
from jax.sharding import PartitionSpec as P

HEAD_SIZE = 128
DOC_MAX = 1024
REACH = 8
ROPE_BASE = 1000000.0
NORM_EPS = 1e-06
HIDDEN = -1e30
Q_TILE = 2
MESH = pl.DeviceIdType.MESH

OWN_Z, OWN_Y, OWN_C, F4_Z, F4_Y, F4_C, F8_Y, F8_C, F2_C, F6_C = range(10)


def norm_rope(block, gain, cos_full, sin_full):
    up = block.astype(jnp.float32)
    mean_square = jnp.mean(up * up, axis=-1, keepdims=True)
    normed = up * lax.rsqrt(mean_square + NORM_EPS) * gain
    swapped = pltpu.roll(normed, HEAD_SIZE // 2, axis=1)
    return (normed * cos_full + swapped * sin_full).astype(jnp.bfloat16)


def kernel(
    count, groups, copies, rows,
    q_hbm, k_hbm, v_hbm, qg_hbm, kg_hbm, freq_hbm, pos_hbm, start_hbm,
    o_ref, win, hidden, q_ref, k_ref, q_rope, qg_ref, kg_ref, freq_ref, pos_ref, start_ref,
    local_sem, in_sem, send_sem, recv_sem,
):
    me = lax.axis_index("sp")
    core = lax.rem(me, 2)
    side = lax.rem(lax.div(me, 2), 2)
    core_peer = me + 1 - 2 * core
    side_peer = me + 2 - 4 * side
    window = (REACH + 1) * rows

    def slot_rows(slot):
        return pl.ds(pl.multiple_of((REACH - slot) * rows, rows), rows)

    def send(kind, g, source, target_slot, target):
        return pltpu.make_async_remote_copy(
            src_ref=win.at[g, :, slot_rows(source)],
            dst_ref=win.at[g, :, slot_rows(target_slot)],
            send_sem=send_sem.at[kind, g],
            recv_sem=recv_sem.at[target_slot, g],
            device_id={"sp": target},
            device_id_type=MESH,
        )

    has_next = me + 4 < count
    f4_slot = 6 - 4 * side

    plan = {
        OWN_Z: (has_next, 0, 4, me + 4),
        OWN_Y: (side == 0, 0, 2, side_peer),
        OWN_C: (core == 0, 0, 1, core_peer),
        F4_Z: ((me >= 4) & has_next, 4, 8, me + 4),
        F4_Y: (me >= 4, 4, f4_slot, side_peer),
        F4_C: (me >= 4, 4, 5 - 2 * core, core_peer),
        F8_Y: ((me >= 8) & (side == 1), 8, 6, side_peer),
        F8_C: ((me >= 8) & (core == 1), 8, 7, core_peer),
        F2_C: (me >= 2, 2, 3 - 2 * core, core_peer),
        F6_C: (me >= 6, 6, 7 - 2 * core, core_peer),
    }

    def start(kind, g):
        condition, source, target_slot, target = plan[kind]

        @pl.when(condition)
        def _():
            send(kind, g, source, target_slot, target).start()

    def arrived(slot, g):
        @pl.when(me >= slot)
        def _():
            send(OWN_Z, g, 0, slot, me).wait_recv()

    value_copies = [
        pltpu.make_async_copy(
            v_hbm.at[:, pl.ds(g * HEAD_SIZE, HEAD_SIZE)],
            win.at[g, 1, pl.ds(REACH * rows, rows)],
            local_sem.at[g],
        )
        for g in range(groups)
    ]
    small = [
        pltpu.make_async_copy(source, target, in_sem.at[i])
        for i, (source, target) in enumerate([
            (k_hbm, k_ref), (kg_hbm, kg_ref), (freq_hbm, freq_ref), (pos_hbm, pos_ref),
            (start_hbm, start_ref), (qg_hbm, qg_ref),
        ])
    ]
    query_copy = pltpu.make_async_copy(q_hbm, q_ref, in_sem.at[6])
    for copy in small + value_copies + [query_copy]:
        copy.start()
    barrier = pltpu.get_barrier_semaphore()
    for peer in (core_peer, side_peer):
        pl.semaphore_signal(barrier, inc=1, device_id={"sp": peer}, device_id_type=MESH)

    @pl.when(has_next)
    def _():
        pl.semaphore_signal(barrier, inc=1, device_id={"sp": me + 4}, device_id_type=MESH)

    @pl.when(me >= 4)
    def _():
        pl.semaphore_signal(barrier, inc=1, device_id={"sp": me - 4}, device_id_type=MESH)

    for copy in small:
        copy.wait()
    places = jnp.broadcast_to(pos_ref[...].astype(jnp.float32), (HEAD_SIZE, rows)).T
    angle = places * freq_ref[...]
    lane = lax.broadcasted_iota(jnp.int32, (rows, HEAD_SIZE), 1)
    cos_full = jnp.cos(angle)
    sine = jnp.sin(angle)
    sin_full = jnp.where(lane < HEAD_SIZE // 2, -sine, sine)
    for g in range(groups):
        win[g, 0, pl.ds(REACH * rows, rows), :] = norm_rope(
            k_ref[:, g * HEAD_SIZE:(g + 1) * HEAD_SIZE], kg_ref[...], cos_full, sin_full
        )

    token = me * rows + lax.broadcasted_iota(jnp.int32, (window, rows), 1)
    key_index = (me - REACH) * rows + lax.broadcasted_iota(jnp.int32, (window, rows), 0)
    visible = (key_index >= start_ref[...]) & (key_index <= token)
    hidden[...] = jnp.where(visible, 0.0, HIDDEN).astype(jnp.bfloat16)

    @pl.loop(0, jnp.maximum(REACH - me, 0))
    def _(j):
        for g in range(groups):
            win[g, :, pl.ds(pl.multiple_of(j * rows, rows), rows), :] = jnp.zeros(
                (2, rows, HEAD_SIZE), jnp.bfloat16
            )

    for copy in value_copies:
        copy.wait()
    inner = (me >= 4) & has_next

    @pl.when(inner)
    def _():
        pl.semaphore_wait(barrier, 4)

    @pl.when(jnp.logical_not(inner))
    def _():
        pl.semaphore_wait(barrier, 3 if count > 4 else 2)

    scale = HEAD_SIZE ** (-0.5) * math.log2(math.e)

    unit = (
        lax.broadcasted_iota(jnp.int32, (rows, rows), 0)
        == lax.broadcasted_iota(jnp.int32, (rows, rows), 1)
    ).astype(jnp.bfloat16)
    units = jnp.concatenate([unit] * Q_TILE, axis=0)

    def columns(g, head):
        return pl.ds(pl.multiple_of((g * copies + head) * HEAD_SIZE, HEAD_SIZE), HEAD_SIZE)

    def attend(g):
        keys = jnp.concatenate([win[g, 0], hidden[...]], axis=1)
        values = jnp.concatenate(
            [win[g, 1], jnp.ones((window, HEAD_SIZE), jnp.bfloat16)], axis=1
        )
        for first in range(0, copies, Q_TILE):
            queries = jnp.concatenate(
                [q_rope[g, first * rows:(first + Q_TILE) * rows], units], axis=1
            )
            scores = lax.dot_general(
                queries, keys, (((1,), (1,)), ((), ())), preferred_element_type=jnp.float32
            )
            row_max = jnp.max(scores, axis=1, keepdims=True)
            weights = jnp.exp2((scores - row_max) * scale).astype(jnp.bfloat16)
            mixed = jnp.dot(weights, values, preferred_element_type=jnp.float32)
            mixed = mixed[:, :HEAD_SIZE] / mixed[:, HEAD_SIZE:]
            for r in range(Q_TILE):
                o_ref[:, columns(g, first + r)] = mixed[r * rows:(r + 1) * rows].astype(
                    jnp.bfloat16
                )

    LEAD = 4
    for g in range(min(LEAD, groups)):
        for kind in (OWN_Z, OWN_Y, OWN_C):
            start(kind, g)

    query_copy.wait()

    @pl.loop(0, groups)
    def _(g):
        for head in range(copies):
            q_rope[g, head * rows:(head + 1) * rows] = norm_rope(
                q_ref[:, columns(g, head)], qg_ref[...], cos_full, sin_full
            )

    @pl.loop(0, groups + 3)
    def _(tick):
        @pl.when(tick + LEAD < groups)
        def _():
            for kind in (OWN_Z, OWN_Y, OWN_C):
                start(kind, tick + LEAD)

        @pl.when(tick < groups)
        def _():
            arrived(4, tick)
            for kind in (F4_Z, F4_Y, F4_C):
                start(kind, tick)

        @pl.when((tick >= 1) & (tick < groups + 1))
        def _():
            arrived(8, tick - 1)
            for kind in (F8_Y, F8_C):
                start(kind, tick - 1)
            arrived(2, tick - 1)
            start(F2_C, tick - 1)

        @pl.when((tick >= 2) & (tick < groups + 2))
        def _():
            arrived(6, tick - 2)
            start(F6_C, tick - 2)

        @pl.when(tick >= 3)
        def _():
            for slot in (1, 3, 5, 7):
                arrived(slot, tick - 3)
            attend(tick - 3)

    @pl.loop(0, groups)
    def _(g):
        for kind, (condition, source, target_slot, target) in plan.items():
            @pl.when(condition)
            def _():
                send(kind, g, source, target_slot, target).wait_send()


def solution(mesh):
    count = mesh.shape["sp"]

    def body(query_proj, key_projection, value_projection, query_gain, key_norm_gain, positions, doc_start):
        rows = query_proj.shape[0]
        groups = key_projection.shape[1] // HEAD_SIZE
        copies = query_proj.shape[1] // key_projection.shape[1]
        assert rows * REACH >= DOC_MAX and count % 4 == 0
        half_dim = HEAD_SIZE // 2
        inv_freq = ROPE_BASE ** (-(np.arange(half_dim) * 2.0 / HEAD_SIZE))
        freq = jnp.asarray(np.concatenate([inv_freq, inv_freq])[None, :], jnp.float32)
        window = (REACH + 1) * rows
        return pl.pallas_call(
            functools.partial(kernel, count, groups, copies, rows),
            out_shape=jax.ShapeDtypeStruct(query_proj.shape, jnp.bfloat16),
            in_specs=[pl.BlockSpec(memory_space=pl.ANY)] * 8,
            out_specs=pl.BlockSpec(memory_space=pltpu.VMEM),
            scratch_shapes=[
                pltpu.VMEM((groups, 2, window, HEAD_SIZE), jnp.bfloat16),
                pltpu.VMEM((window, rows), jnp.bfloat16),
                pltpu.VMEM(query_proj.shape, jnp.bfloat16),
                pltpu.VMEM(key_projection.shape, jnp.bfloat16),
                pltpu.VMEM((groups, copies * rows, HEAD_SIZE), jnp.bfloat16),
                pltpu.VMEM((1, HEAD_SIZE), jnp.float32),
                pltpu.VMEM((1, HEAD_SIZE), jnp.float32),
                pltpu.VMEM((1, HEAD_SIZE), jnp.float32),
                pltpu.VMEM((1, rows), jnp.int32),
                pltpu.VMEM((1, rows), jnp.int32),
                pltpu.SemaphoreType.DMA((groups,)),
                pltpu.SemaphoreType.DMA((7,)),
                pltpu.SemaphoreType.DMA((10, groups)),
                pltpu.SemaphoreType.DMA((REACH + 1, groups)),
            ],
            compiler_params=pltpu.CompilerParams(
                collective_id=0, has_side_effects=True, vmem_limit_bytes=60 * 1024 * 1024
            ),
        )(
            query_proj, key_projection, value_projection,
            query_gain[None, :], key_norm_gain[None, :], freq, positions[None, :], doc_start[None, :],
        )

    tokens = P(("dp", "sp"), None)
    vector = P(("dp", "sp"))
    return jax.shard_map(
        body,
        mesh=mesh,
        in_specs=(tokens, tokens, tokens, P(), P(), vector, vector),
        out_specs=tokens,
        check_vma=False,
    )
```

profile of v0, /device:TPU:16, one launch (start us, length us, event | category | flops | bytes accessed | tf_op | source)
XLA Modules:
  0.0 47.4 jit_solution(15209182783846770319)
XLA Ops:
  0.0 44.3 %shard_map.82 = bf16[128,8192]{1,0:T(8,128)(2,1)} custom-call(bf16[128,8192]{1,0:T(8,128)(2,1)} %q_hbm.1, bf16[128,1024]{1,0:T(8,128)(2,1)} %k_hbm.1, bf16[128,1024]{1,0:T(8,128)(2,1)} %v_hbm.1, f32[1,128]{1,0:T(1,128)} %bitcast.4, f32[1,128]{1,0:T(1,128)} %bitcast.5, f32[1,128]{1,0:T(1,128)} %constant.2.clone.freq_hbm, s32[1,128]{1,0:T(1,128)} %bitcast.6, ...), custom_call_target="tpu_custom_call" | custom-call | tf_op jit(solution)/shard_map/pallas_call | solution.py:251
  44.3 3.1 %copy.10 = bf16[128,8192]{1,0:T(8,128)(2,1)} copy(bf16[128,8192]{1,0:T(8,128)(2,1)} %shard_map.82) | data formatting | bytes 4194304
where the time goes:
time: 47.6 us; the launch traced here: 47.4 us
  Pallas kernels  44.3 us (93%)
  local copies, waits for them, and re-layouts  3.1 us (7%)
    pallas_call x1, Pallas kernels, body(): pl.pallas_call(functools.partial(kernel, count, groups, copies, rows), ou...  44.3 us
    unnamed x1, local copies, waits for them, and re-layouts  3.1 us

commit v1 on v0

v1 whole, which is shorter than its diff:
```python
import functools
import math

import jax
import jax.numpy as jnp
import numpy as np
from jax import lax
from jax.experimental import pallas as pl
from jax.experimental.pallas import tpu as pltpu
from jax.sharding import PartitionSpec as P

HEAD_SIZE = 128
DOC_MAX = 1024
REACH = 8
ROPE_BASE = 1000000.0
NORM_EPS = 1e-06
HIDDEN = -1e30
Q_TILE = 2
LEAD = 5
MESH = pl.DeviceIdType.MESH

KEY, VALUE = 0, 1
OWN_Z, OWN_Y, OWN_C, F4_Z, F4_Y, F4_C, F8_Y, F8_C, F2_C, F6_C = range(10)


def norm_rope(block, swap, straight, crossed):
    up = block.astype(jnp.float32)
    mean_square = jnp.mean(up * up, axis=-1, keepdims=True)
    swapped = jnp.dot(block, swap, preferred_element_type=jnp.float32)
    return (up * straight + swapped * crossed) * lax.rsqrt(mean_square + NORM_EPS)


def chunk_order(groups):
    head = min(2, groups)
    order = [(VALUE, g) for g in range(head)] + [(KEY, g) for g in range(head)]
    for g in range(head, groups):
        order += [(KEY, g), (VALUE, g)]
    return order


def kernel(
    count, groups, copies, rows,
    q_hbm, k_hbm, v_hbm, qg_hbm, kg_hbm, freq_hbm, pos_hbm, start_hbm,
    o_hbm, win_k, win_v, hidden, q_ref, k_ref, q_rope, o_ref,
    scores_a, scores_b, top_a, top_b, weights_0, weights_1, weights_2, weights_3,
    qg_ref, kg_ref, freq_ref, pos_ref, start_ref,
    value_sem, in_sem, query_sem, out_sem, send_sem, recv_sem,
):
    me = lax.axis_index("sp")
    core = lax.rem(me, 2)
    side = lax.rem(lax.div(me, 2), 2)
    core_peer = me + 1 - 2 * core
    side_peer = me + 2 - 4 * side
    blocks = REACH + 1
    scores_buf = [scores_a, scores_b]
    top_buf = [top_a, top_b]
    weights_buf = [weights_0, weights_1, weights_2, weights_3]
    tiles = copies // Q_TILE
    tile_rows = Q_TILE * rows

    def chunk(c, g, slot):
        return (win_k, win_v)[c].at[g, REACH - slot]

    def send(kind, c, g, source, target_slot, target):
        return pltpu.make_async_remote_copy(
            src_ref=chunk(c, g, source),
            dst_ref=chunk(c, g, target_slot),
            send_sem=send_sem.at[c, kind],
            recv_sem=recv_sem.at[c, target_slot, g],
            device_id={"sp": target},
            device_id_type=MESH,
        )

    has_next = me + 4 < count
    f4_slot = 6 - 4 * side

    plan = {
        OWN_Z: (has_next, 0, 4, me + 4),
        OWN_Y: (side == 0, 0, 2, side_peer),
        OWN_C: (core == 0, 0, 1, core_peer),
        F4_Z: ((me >= 4) & has_next, 4, 8, me + 4),
        F4_Y: (me >= 4, 4, f4_slot, side_peer),
        F4_C: (me >= 4, 4, 5 - 2 * core, core_peer),
        F8_Y: ((me >= 8) & (side == 1), 8, 6, side_peer),
        F8_C: ((me >= 8) & (core == 1), 8, 7, core_peer),
        F2_C: (me >= 2, 2, 3 - 2 * core, core_peer),
        F6_C: (me >= 6, 6, 7 - 2 * core, core_peer),
    }

    def start(kind, c, g):
        condition, source, target_slot, target = plan[kind]

        @pl.when(condition)
        def _():
            send(kind, c, g, source, target_slot, target).start()

    def arrived(slot, c, g):
        @pl.when(me >= slot)
        def _():
            send(OWN_Z, c, g, 0, slot, me).wait_recv()

    def own(c, g):
        for kind in (OWN_Z, OWN_Y, OWN_C):
            start(kind, c, g)

    forwards = {4: (F4_Z, F4_Y, F4_C), 8: (F8_Y, F8_C), 2: (F2_C,), 6: (F6_C,)}

    def relay(slot, c, g):
        arrived(slot, c, g)
        for kind in forwards[slot]:
            start(kind, c, g)

    value_copies = [
        pltpu.make_async_copy(
            v_hbm.at[:, pl.ds(g * HEAD_SIZE, HEAD_SIZE)],
            win_v.at[g, REACH],
            value_sem.at[g],
        )
        for g in range(groups)
    ]
    small = [
        pltpu.make_async_copy(source, target, in_sem.at[i])
        for i, (source, target) in enumerate([
            (pos_hbm, pos_ref), (freq_hbm, freq_ref), (kg_hbm, kg_ref), (k_hbm, k_ref),
            (start_hbm, start_ref), (qg_hbm, qg_ref),
        ])
    ]
    width = copies * HEAD_SIZE
    query_copies = [
        pltpu.make_async_copy(
            q_hbm.at[:, pl.ds(i * HEAD_SIZE, HEAD_SIZE)], q_ref.at[i], query_sem.at[i // copies]
        )
        for i in range(groups * copies)
    ]
    barrier = pltpu.get_barrier_semaphore()
    for peer in (core_peer, side_peer):
        pl.semaphore_signal(barrier, inc=1, device_id={"sp": peer}, device_id_type=MESH)

    @pl.when(has_next)
    def _():
        pl.semaphore_signal(barrier, inc=1, device_id={"sp": me + 4}, device_id_type=MESH)

    @pl.when(me >= 4)
    def _():
        pl.semaphore_signal(barrier, inc=1, device_id={"sp": me - 4}, device_id_type=MESH)

    for copy in value_copies[:2] + small + value_copies[2:] + query_copies:
        copy.start()

    order = chunk_order(groups)
    head = min(2, groups)
    for copy in value_copies[:head]:
        copy.wait()
    inner = (me >= 4) & has_next

    @pl.when(inner)
    def _():
        pl.semaphore_wait(barrier, 4)

    @pl.when(jnp.logical_not(inner))
    def _():
        pl.semaphore_wait(barrier, 3 if count > 4 else 2)

    for n in range(head):
        own(*order[n])

    for copy in small:
        copy.wait()
    places = jnp.broadcast_to(pos_ref[...].astype(jnp.float32), (HEAD_SIZE, rows)).T
    angle = places * freq_ref[...]
    lane = lax.broadcasted_iota(jnp.int32, (rows, HEAD_SIZE), 1)
    cos_full = jnp.cos(angle)
    sine = jnp.sin(angle)
    sin_full = jnp.where(lane < HEAD_SIZE // 2, -sine, sine)
    swap = (
        lax.rem(lax.broadcasted_iota(jnp.int32, (HEAD_SIZE, HEAD_SIZE), 0) + HEAD_SIZE // 2, HEAD_SIZE)
        == lax.broadcasted_iota(jnp.int32, (HEAD_SIZE, HEAD_SIZE), 1)
    ).astype(jnp.bfloat16)

    def tables(gain_ref):
        gain = jnp.broadcast_to(gain_ref[...], (rows, HEAD_SIZE))
        return gain * cos_full, pltpu.roll(gain, HEAD_SIZE // 2, axis=1) * sin_full

    straight, crossed = tables(kg_ref)
    for g in range(groups):
        rotated = norm_rope(k_ref[:, g * HEAD_SIZE:(g + 1) * HEAD_SIZE], swap, straight, crossed)
        win_k[g, REACH] = rotated.T.astype(jnp.bfloat16)
    straight, crossed = tables(qg_ref)

    for copy in value_copies[head:]:
        copy.wait()
    for n in range(head, min(LEAD, 2 * groups)):
        own(*order[n])

    starts = jnp.broadcast_to(start_ref[...], (rows, rows)).T
    token = me * rows + lax.broadcasted_iota(jnp.int32, (rows, rows), 0)
    for b in range(REACH + 1):
        key_index = (me - REACH + b) * rows + lax.broadcasted_iota(jnp.int32, (rows, rows), 1)
        visible = (key_index >= starts) & (key_index <= token)
        hidden[b] = jnp.where(visible, 0.0, HIDDEN).astype(jnp.bfloat16)

    @pl.loop(0, jnp.maximum(REACH - me, 0))
    def _(j):
        for g in range(groups):
            win_k[g, j] = jnp.zeros((HEAD_SIZE, rows), jnp.bfloat16)
            win_v[g, j] = jnp.zeros((rows, HEAD_SIZE), jnp.bfloat16)

    weights_buf[tiles - 1][...] = jnp.zeros((blocks, tile_rows, rows), jnp.bfloat16)

    scale = HEAD_SIZE ** (-0.5) * math.log2(math.e)
    unit = (
        lax.broadcasted_iota(jnp.int32, (rows, rows), 0)
        == lax.broadcasted_iota(jnp.int32, (rows, rows), 1)
    ).astype(jnp.bfloat16)
    units = jnp.concatenate([unit] * Q_TILE, axis=0)

    def prepare(g):
        at = pl.ds(g * width, width)
        pltpu.make_async_copy(q_hbm.at[:, at], q_hbm.at[:, at], query_sem.at[g]).wait()
        for head_index in range(copies):
            q_rope[g, head_index * rows:(head_index + 1) * rows] = norm_rope(
                q_ref[g * copies + head_index], swap, straight, crossed
            ).astype(jnp.bfloat16)

    def score(g, tile):
        queries = jnp.concatenate(
            [q_rope[g, tile * tile_rows:(tile + 1) * tile_rows], units], axis=1
        )
        best = None
        for b in range(0, blocks, 2):
            pair = range(b, min(b + 2, blocks))
            keys = jnp.concatenate([
                jnp.concatenate([win_k[g, i] for i in pair], axis=1),
                jnp.concatenate([hidden[i] for i in pair], axis=1),
            ], axis=0)
            part = jnp.dot(queries, keys, preferred_element_type=jnp.float32)
            for at, i in enumerate(pair):
                piece = part[:, at * rows:(at + 1) * rows]
                scores_buf[tile % 2][i] = piece
                best = piece if best is None else jnp.maximum(best, piece)
        top = jnp.max(best, axis=1, keepdims=True)
        top_buf[tile % 2][...] = jnp.broadcast_to(top, (tile_rows, rows))

    def soften(tile):
        top = top_buf[tile % 2][...]
        for b in range(blocks):
            part = scores_buf[tile % 2][b]
            weights_buf[tile][b] = jnp.exp2((part - top) * scale).astype(jnp.bfloat16)

    def mix(g, tile):
        values = jnp.concatenate([
            win_v[g].reshape(blocks * rows, HEAD_SIZE),
            jnp.ones((blocks * rows, HEAD_SIZE), jnp.bfloat16),
        ], axis=1)
        weights = jnp.concatenate([weights_buf[tile][b] for b in range(blocks)], axis=1)
        mixed = jnp.dot(weights, values, preferred_element_type=jnp.float32)
        mixed = mixed[:, :HEAD_SIZE] / mixed[:, HEAD_SIZE:]
        for r in range(Q_TILE):
            o_ref[g * copies + tile * Q_TILE + r] = mixed[r * rows:(r + 1) * rows].astype(jnp.bfloat16)

    def result_start(g):
        for i in range(copies):
            head_index = g * copies + i
            at = pl.ds(pl.multiple_of(head_index * HEAD_SIZE, HEAD_SIZE), HEAD_SIZE)
            pltpu.make_async_copy(o_ref.at[head_index], o_hbm.at[:, at], out_sem.at[g]).start()

    def result_wait(g):
        at = pl.ds(g * width, width)
        pltpu.make_async_copy(o_hbm.at[:, at], o_hbm.at[:, at], out_sem.at[g]).wait()

    total = 2 * groups
    first_step = 16.8

    def arrival(slot, n):
        four = n + 3.4 if n < LEAD else 2 * n - LEAD + 4.4
        eight = min(2 * n + LEAD + 3.4, 2 * total + 2.4 - (total - 1 - n))
        return {4: four, 2: four + 2.9, 8: eight, 6: eight + 3.0}[slot]

    early = sorted(
        (arrival(slot, n), slot, n) for slot in (4, 2, 8, 6) for n in range(total)
    )
    late = [event for event in early if event[0] >= first_step]
    early = [event for event in early if event[0] < first_step]

    def event(slot, n):
        relay(slot, *order[n])
        if slot == 4 and n + LEAD < total:
            own(*order[n + LEAD])

    for g in range(min(2, groups)):
        prepare(g)
    ready = min(2, groups)
    for at, (_, slot, n) in enumerate(early):
        event(slot, n)
        if at % 2 == 1 and ready < groups:
            prepare(ready)
            ready += 1
    for g in range(ready, groups):
        prepare(g)

    by_tile = {}
    for when, slot, n in late:
        step = max(0, min(int(when - first_step), groups * tiles - 1))
        by_tile.setdefault(step, []).append((slot, n))

    def near(c, g):
        for slot in (1, 3, 5, 7):
            arrived(slot, c, g)

    near(KEY, 0)
    score(0, 0)

    def relays(g, tile):
        for (kind_step, todo) in by_tile.items():
            if kind_step % tiles != tile:
                continue

            @pl.when(g == kind_step // tiles)
            def _():
                for slot, n in todo:
                    event(slot, n)

    @pl.loop(0, groups - 1)
    def _(g):
        for tile in range(tiles):
            relays(g, tile)
            if tile == 0:
                near(VALUE, g)
            if tile == tiles - 1:
                near(KEY, g + 1)
                score(g + 1, 0)
            else:
                score(g, tile + 1)
            soften(tile)
            if tile == 0:
                mix(jnp.maximum(g - 1, 0), tiles - 1)

                @pl.when(g > 0)
                def _():
                    result_start(g - 1)
            else:
                mix(g, tile - 1)

    last = groups - 1
    for tile in range(tiles):
        relays(last, tile)
        if tile < tiles - 1:
            score(last, tile + 1)
        soften(tile)
        if tile == 0:
            mix(max(last - 1, 0), tiles - 1)
            if last > 0:
                result_start(last - 1)
    near(VALUE, last)
    for tile in range(tiles):
        mix(last, tile)
    result_start(last)

    for c in (KEY, VALUE):
        whole = (win_k, win_v)[c].at[:, REACH]
        for kind, (condition, _, _, target) in plan.items():
            @pl.when(condition)
            def _():
                pltpu.make_async_remote_copy(
                    src_ref=whole, dst_ref=whole, send_sem=send_sem.at[c, kind],
                    recv_sem=recv_sem.at[c, 0, 0], device_id={"sp": target}, device_id_type=MESH,
                ).wait_send()

    for g in range(groups):
        result_wait(g)


def solution(mesh):
    count = mesh.shape["sp"]

    def body(query_proj, key_projection, value_projection, query_gain, key_norm_gain, positions, doc_start):
        rows = query_proj.shape[0]
        groups = key_projection.shape[1] // HEAD_SIZE
        copies = query_proj.shape[1] // key_projection.shape[1]
        assert rows * REACH >= DOC_MAX and count % 4 == 0
        half_dim = HEAD_SIZE // 2
        inv_freq = ROPE_BASE ** (-(np.arange(half_dim) * 2.0 / HEAD_SIZE))
        freq = jnp.asarray(np.concatenate([inv_freq, inv_freq])[None, :], jnp.float32)
        blocks = REACH + 1
        tile_rows = Q_TILE * rows
        return pl.pallas_call(
            functools.partial(kernel, count, groups, copies, rows),
            out_shape=jax.ShapeDtypeStruct(query_proj.shape, jnp.bfloat16),
            in_specs=[pl.BlockSpec(memory_space=pl.ANY)] * 8,
            out_specs=pl.BlockSpec(memory_space=pl.ANY),
            scratch_shapes=[
                pltpu.VMEM((groups, blocks, HEAD_SIZE, rows), jnp.bfloat16),
                pltpu.VMEM((groups, blocks, rows, HEAD_SIZE), jnp.bfloat16),
                pltpu.VMEM((blocks, rows, rows), jnp.bfloat16),
                pltpu.VMEM((groups * copies, rows, HEAD_SIZE), jnp.bfloat16),
                pltpu.VMEM(key_projection.shape, jnp.bfloat16),
                pltpu.VMEM((groups, copies * rows, HEAD_SIZE), jnp.bfloat16),
                pltpu.VMEM((groups * copies, rows, HEAD_SIZE), jnp.bfloat16),
                pltpu.VMEM((blocks, tile_rows, rows), jnp.float32),
                pltpu.VMEM((blocks, tile_rows, rows), jnp.float32),
                pltpu.VMEM((tile_rows, rows), jnp.float32),
                pltpu.VMEM((tile_rows, rows), jnp.float32),
                pltpu.VMEM((blocks, tile_rows, rows), jnp.bfloat16),
                pltpu.VMEM((blocks, tile_rows, rows), jnp.bfloat16),
                pltpu.VMEM((blocks, tile_rows, rows), jnp.bfloat16),
                pltpu.VMEM((blocks, tile_rows, rows), jnp.bfloat16),
                pltpu.VMEM((1, HEAD_SIZE), jnp.float32),
                pltpu.VMEM((1, HEAD_SIZE), jnp.float32),
                pltpu.VMEM((1, HEAD_SIZE), jnp.float32),
                pltpu.VMEM((1, rows), jnp.int32),
                pltpu.VMEM((1, rows), jnp.int32),
                pltpu.SemaphoreType.DMA((groups,)),
                pltpu.SemaphoreType.DMA((6,)),
                pltpu.SemaphoreType.DMA((groups,)),
                pltpu.SemaphoreType.DMA((groups,)),
                pltpu.SemaphoreType.DMA((2, 10)),
                pltpu.SemaphoreType.DMA((2, REACH + 1, groups)),
            ],
            compiler_params=pltpu.CompilerParams(
                collective_id=0, has_side_effects=True, vmem_limit_bytes=60 * 1024 * 1024
            ),
        )(
            query_proj, key_projection, value_projection,
            query_gain[None, :], key_norm_gain[None, :], freq, positions[None, :], doc_start[None, :],
        )

    tokens = P(("dp", "sp"), None)
    vector = P(("dp", "sp"))
    return jax.shard_map(
        body,
        mesh=mesh,
        in_specs=(tokens, tokens, tokens, P(), P(), vector, vector),
        out_specs=tokens,
        check_vma=False,
    )
```

time: 47.6 us -> 46.9 us (0.985); the launches traced: 47.4 us -> 46.1 us
  Pallas kernels: 44.3 us -> 43 us
    pallas_call x1, Pallas kernels: 44.3 us -> 43 us  [body(): pl.pallas_call(functools.partial(kernel, count, groups, copies, rows), ou...]
where the time goes in v1:
time: 46.9 us; the launch traced here: 46.1 us
  Pallas kernels  43 us (92%)
  local copies, waits for them, and re-layouts  3.1 us (7%)
    pallas_call x1, Pallas kernels, body(): pl.pallas_call(functools.partial(kernel, count, groups, copies, rows), ou...  43 us
    unnamed x1, local copies, waits for them, and re-layouts  3.1 us

profile of v1, /device:TPU:16, one launch (start us, length us, event | category | flops | bytes accessed | tf_op | source)
XLA Modules:
  0.0 46.1 jit_solution(6987450771925996059)
XLA Ops:
  0.0 43.0 %shard_map.82 = bf16[128,8192]{1,0:T(8,128)(2,1)} custom-call(bf16[128,8192]{1,0:T(8,128)(2,1)} %q_hbm.1, bf16[128,1024]{1,0:T(8,128)(2,1)} %k_hbm.1, bf16[128,1024]{1,0:T(8,128)(2,1)} %v_hbm.1, f32[1,128]{1,0:T(1,128)} %bitcast.4, f32[1,128]{1,0:T(1,128)} %bitcast.5, f32[1,128]{1,0:T(1,128)} %constant.2.clone.freq_hbm, s32[1,128]{1,0:T(1,128)} %bitcast.6, ...), custom_call_target="tpu_custom_call" | custom-call | tf_op jit(solution)/shard_map/pallas_call | solution.py:386
  43.0 3.1 %copy.10 = bf16[128,8192]{1,0:T(8,128)(2,1)} copy(bf16[128,8192]{1,0:T(8,128)(2,1)} %shard_map.82) | data formatting | bytes 4194304

commit v2 on v1

--- a/solution.py
+++ b/solution.py
@@ -15,7 +15,7 @@
 ROPE_BASE = 1000000.0
 NORM_EPS = 1e-06
 HIDDEN = -1e30
-Q_TILE = 2
+Q_TILE = 4
 LEAD = 5
 MESH = pl.DeviceIdType.MESH
 
@@ -42,7 +42,7 @@
     count, groups, copies, rows,
     q_hbm, k_hbm, v_hbm, qg_hbm, kg_hbm, freq_hbm, pos_hbm, start_hbm,
     o_hbm, win_k, win_v, hidden, q_ref, k_ref, q_rope, o_ref,
-    scores_a, scores_b, top_a, top_b, weights_0, weights_1, weights_2, weights_3,
+    scores_a, scores_b, top_a, top_b, weights_0, weights_1,
     qg_ref, kg_ref, freq_ref, pos_ref, start_ref,
     value_sem, in_sem, query_sem, out_sem, send_sem, recv_sem,
 ):
@@ -54,7 +54,7 @@
     blocks = REACH + 1
     scores_buf = [scores_a, scores_b]
     top_buf = [top_a, top_b]
-    weights_buf = [weights_0, weights_1, weights_2, weights_3]
+    weights_buf = [weights_0, weights_1]
     tiles = copies // Q_TILE
     tile_rows = Q_TILE * rows
 
@@ -238,11 +238,10 @@
                 piece = part[:, at * rows:(at + 1) * rows]
                 scores_buf[tile % 2][i] = piece
                 best = piece if best is None else jnp.maximum(best, piece)
-        top = jnp.max(best, axis=1, keepdims=True)
-        top_buf[tile % 2][...] = jnp.broadcast_to(top, (tile_rows, rows))
+        top_buf[tile % 2][...] = best
 
     def soften(tile):
-        top = top_buf[tile % 2][...]
+        top = jnp.max(top_buf[tile % 2][...], axis=1, keepdims=True)
         for b in range(blocks):
             part = scores_buf[tile % 2][b]
             weights_buf[tile][b] = jnp.exp2((part - top) * scale).astype(jnp.bfloat16)
@@ -300,13 +299,14 @@
 
     by_tile = {}
     for when, slot, n in late:
-        step = max(0, min(int(when - first_step), groups * tiles - 1))
+        step = max(0, min(int((when - first_step) * tiles / 4), groups * tiles - 1))
         by_tile.setdefault(step, []).append((slot, n))
 
     def near(c, g):
         for slot in (1, 3, 5, 7):
             arrived(slot, c, g)
 
+    near(VALUE, 0)
     near(KEY, 0)
     score(0, 0)
 
@@ -324,8 +324,10 @@
     def _(g):
         for tile in range(tiles):
             relays(g, tile)
-            if tile == 0:
-                near(VALUE, g)
+            if tile == 1:
+                @pl.when(g > 0)
+                def _():
+                    near(VALUE, g)
             if tile == tiles - 1:
                 near(KEY, g + 1)
                 score(g + 1, 0)
@@ -402,8 +404,6 @@
                 pltpu.VMEM((tile_rows, rows), jnp.float32),
                 pltpu.VMEM((blocks, tile_rows, rows), jnp.bfloat16),
                 pltpu.VMEM((blocks, tile_rows, rows), jnp.bfloat16),
-                pltpu.VMEM((blocks, tile_rows, rows), jnp.bfloat16),
-                pltpu.VMEM((blocks, tile_rows, rows), jnp.bfloat16),
                 pltpu.VMEM((1, HEAD_SIZE), jnp.float32),
                 pltpu.VMEM((1, HEAD_SIZE), jnp.float32),
                 pltpu.VMEM((1, HEAD_SIZE), jnp.float32),

time: 46.9 us -> 42.5 us (0.906); the launches traced: 46.1 us -> 42.4 us
  Pallas kernels: 43 us -> 39.3 us
    pallas_call x1, Pallas kernels: 43 us -> 39.3 us  [body(): pl.pallas_call(functools.partial(kernel, count, groups, copies, rows), ou...]
where the time goes in v2:
time: 42.5 us; the launch traced here: 42.4 us
  Pallas kernels  39.3 us (92%)
  local copies, waits for them, and re-layouts  3.1 us (7%)
    pallas_call x1, Pallas kernels, body(): pl.pallas_call(functools.partial(kernel, count, groups, copies, rows), ou...  39.3 us
    unnamed x1, local copies, waits for them, and re-layouts  3.1 us

profile of v2, /device:TPU:16, one launch (start us, length us, event | category | flops | bytes accessed | tf_op | source)
XLA Modules:
  0.0 42.4 jit_solution(3482623911502724288)
XLA Ops:
  0.0 39.3 %shard_map.82 = bf16[128,8192]{1,0:T(8,128)(2,1)} custom-call(bf16[128,8192]{1,0:T(8,128)(2,1)} %q_hbm.1, bf16[128,1024]{1,0:T(8,128)(2,1)} %k_hbm.1, bf16[128,1024]{1,0:T(8,128)(2,1)} %v_hbm.1, f32[1,128]{1,0:T(1,128)} %bitcast.4, f32[1,128]{1,0:T(1,128)} %bitcast.5, f32[1,128]{1,0:T(1,128)} %constant.2.clone.freq_hbm, s32[1,128]{1,0:T(1,128)} %bitcast.6, ...), custom_call_target="tpu_custom_call" | custom-call | tf_op jit(solution)/shard_map/pallas_call | solution.py:388
  39.3 3.1 %copy.10 = bf16[128,8192]{1,0:T(8,128)(2,1)} copy(bf16[128,8192]{1,0:T(8,128)(2,1)} %shard_map.82) | data formatting | bytes 4194304

commit v3 on v2

--- a/solution.py
+++ b/solution.py
@@ -41,10 +41,10 @@
 def kernel(
     count, groups, copies, rows,
     q_hbm, k_hbm, v_hbm, qg_hbm, kg_hbm, freq_hbm, pos_hbm, start_hbm,
-    o_hbm, win_k, win_v, hidden, q_ref, k_ref, q_rope, o_ref,
+    o_ref, win_k, win_v, hidden, q_ref, k_ref, q_rope,
     scores_a, scores_b, top_a, top_b, weights_0, weights_1,
     qg_ref, kg_ref, freq_ref, pos_ref, start_ref,
-    value_sem, in_sem, query_sem, out_sem, send_sem, recv_sem,
+    value_sem, in_sem, query_sem, send_sem, recv_sem,
 ):
     me = lax.axis_index("sp")
     core = lax.rem(me, 2)
@@ -257,16 +257,6 @@
         for r in range(Q_TILE):
             o_ref[g * copies + tile * Q_TILE + r] = mixed[r * rows:(r + 1) * rows].astype(jnp.bfloat16)
 
-    def result_start(g):
-        for i in range(copies):
-            head_index = g * copies + i
-            at = pl.ds(pl.multiple_of(head_index * HEAD_SIZE, HEAD_SIZE), HEAD_SIZE)
-            pltpu.make_async_copy(o_ref.at[head_index], o_hbm.at[:, at], out_sem.at[g]).start()
-
-    def result_wait(g):
-        at = pl.ds(g * width, width)
-        pltpu.make_async_copy(o_hbm.at[:, at], o_hbm.at[:, at], out_sem.at[g]).wait()
-
     total = 2 * groups
     first_step = 16.8
 
@@ -336,10 +326,6 @@
             soften(tile)
             if tile == 0:
                 mix(jnp.maximum(g - 1, 0), tiles - 1)
-
-                @pl.when(g > 0)
-                def _():
-                    result_start(g - 1)
             else:
                 mix(g, tile - 1)
 
@@ -351,12 +337,9 @@
         soften(tile)
         if tile == 0:
             mix(max(last - 1, 0), tiles - 1)
-            if last > 0:
-                result_start(last - 1)
     near(VALUE, last)
     for tile in range(tiles):
         mix(last, tile)
-    result_start(last)
 
     for c in (KEY, VALUE):
         whole = (win_k, win_v)[c].at[:, REACH]
@@ -368,8 +351,12 @@
                     recv_sem=recv_sem.at[c, 0, 0], device_id={"sp": target}, device_id_type=MESH,
                 ).wait_send()
 
-    for g in range(groups):
-        result_wait(g)
+
+def leave(heads_ref, o_hbm, sem):
+    for i in range(heads_ref.shape[0]):
+        at = pl.ds(i * HEAD_SIZE, HEAD_SIZE)
+        pltpu.make_async_copy(heads_ref.at[i], o_hbm.at[:, at], sem).start()
+    pltpu.make_async_copy(o_hbm, o_hbm, sem).wait()
 
 
 def solution(mesh):
@@ -385,11 +372,11 @@
         freq = jnp.asarray(np.concatenate([inv_freq, inv_freq])[None, :], jnp.float32)
         blocks = REACH + 1
         tile_rows = Q_TILE * rows
-        return pl.pallas_call(
+        heads = pl.pallas_call(
             functools.partial(kernel, count, groups, copies, rows),
-            out_shape=jax.ShapeDtypeStruct(query_proj.shape, jnp.bfloat16),
+            out_shape=jax.ShapeDtypeStruct((groups * copies, rows, HEAD_SIZE), jnp.bfloat16),
             in_specs=[pl.BlockSpec(memory_space=pl.ANY)] * 8,
-            out_specs=pl.BlockSpec(memory_space=pl.ANY),
+            out_specs=pl.BlockSpec(memory_space=pltpu.VMEM),
             scratch_shapes=[
                 pltpu.VMEM((groups, blocks, HEAD_SIZE, rows), jnp.bfloat16),
                 pltpu.VMEM((groups, blocks, rows, HEAD_SIZE), jnp.bfloat16),
@@ -397,7 +384,6 @@
                 pltpu.VMEM((groups * copies, rows, HEAD_SIZE), jnp.bfloat16),
                 pltpu.VMEM(key_projection.shape, jnp.bfloat16),
                 pltpu.VMEM((groups, copies * rows, HEAD_SIZE), jnp.bfloat16),
-                pltpu.VMEM((groups * copies, rows, HEAD_SIZE), jnp.bfloat16),
                 pltpu.VMEM((blocks, tile_rows, rows), jnp.float32),
                 pltpu.VMEM((blocks, tile_rows, rows), jnp.float32),
                 pltpu.VMEM((tile_rows, rows), jnp.float32),
@@ -412,17 +398,26 @@
                 pltpu.SemaphoreType.DMA((groups,)),
                 pltpu.SemaphoreType.DMA((6,)),
                 pltpu.SemaphoreType.DMA((groups,)),
-                pltpu.SemaphoreType.DMA((groups,)),
                 pltpu.SemaphoreType.DMA((2, 10)),
                 pltpu.SemaphoreType.DMA((2, REACH + 1, groups)),
             ],
             compiler_params=pltpu.CompilerParams(
-                collective_id=0, has_side_effects=True, vmem_limit_bytes=60 * 1024 * 1024
+                collective_id=0, has_side_effects=True, vmem_limit_bytes=41943040
             ),
         )(
-            query_proj, key_projection, value_projection,
-            query_gain[None, :], key_norm_gain[None, :], freq, positions[None, :], doc_start[None, :],
+            *(pltpu.with_memory_space_constraint(array, pltpu.HBM) for array in (
+                query_proj, key_projection, value_projection,
+                query_gain[None, :], key_norm_gain[None, :], freq, positions[None, :], doc_start[None, :],
+            ))
         )
+        return pl.pallas_call(
+            leave,
+            out_shape=jax.ShapeDtypeStruct(query_proj.shape, jnp.bfloat16),
+            in_specs=[pl.BlockSpec(memory_space=pltpu.VMEM)],
+            out_specs=pl.BlockSpec(memory_space=pl.ANY),
+            scratch_shapes=[pltpu.SemaphoreType.DMA],
+            compiler_params=pltpu.CompilerParams(vmem_limit_bytes=8 * 1024 * 1024),
+        )(heads)
 
     tokens = P(("dp", "sp"), None)
     vector = P(("dp", "sp"))

time: 42.5 us -> 40 us (0.941)
  local copies, waits for them, and re-layouts: 3.1 us -> 0 us
  Pallas kernels: 39.3 us -> 39.8 us
    unnamed x1 -> x0, local copies, waits for them, and re-layouts: 3.1 us -> none
    pallas_call x0 -> x1, Pallas kernels: none -> 1.29 us  [body(): pl.pallas_call(leave, out_shape=jax.ShapeDtypeStruct(query_proj.shape, jn...]
    pallas_call x1, Pallas kernels: 39.3 us -> 38.5 us  [body(): pl.pallas_call(functools.partial(kernel, count, groups, copies, rows), ou...]
where the time goes in v3:
time: 40 us; the launch traced here: 39.8 us
  Pallas kernels  39.8 us (99%)
    pallas_call x1, Pallas kernels, body(): pl.pallas_call(functools.partial(kernel, count, groups, copies, rows), ou...  38.5 us
    pallas_call x1, Pallas kernels, body(): pl.pallas_call(leave, out_shape=jax.ShapeDtypeStruct(query_proj.shape, jn...  1.29 us

profile of v3, /device:TPU:16, one launch (start us, length us, event | category | flops | bytes accessed | tf_op | source)
XLA Modules:
  0.0 39.8 jit_solution(2722750777553645199)
XLA Ops:
  0.0 38.5 %shard_map.82.heads_ref = bf16[64,128,128]{2,1,0:T(8,128)(2,1)S(1)} custom-call(bf16[128,8192]{1,0:T(8,128)(2,1)} %q_hbm.1, bf16[128,1024]{1,0:T(8,128)(2,1)} %k_hbm.1, bf16[128,1024]{1,0:T(8,128)(2,1)} %v_hbm.1, f32[1,128]{1,0:T(1,128)} %bitcast.4, f32[1,128]{1,0:T(1,128)} %bitcast.5, f32[1,128]{1,0:T(1,128)} %constant.2.clone.freq_hbm, s32[1,128]{1,0:T(1,128)} %bitcast.6, ...), custom_call_target="tpu_custom_call" | custom-call | tf_op jit(solution)/shard_map/pallas_call | solution.py:375
  38.5 1.3 %shard_map.83 = bf16[128,8192]{1,0:T(8,128)(2,1)} custom-call(bf16[64,128,128]{2,1,0:T(8,128)(2,1)S(1)} %shard_map.82.heads_ref), custom_call_target="tpu_custom_call" | custom-call | tf_op jit(solution)/shard_map/pallas_call | solution.py:413

commit v4 on v3

--- a/solution.py
+++ b/solution.py
@@ -16,11 +16,12 @@
 NORM_EPS = 1e-06
 HIDDEN = -1e30
 Q_TILE = 4
-LEAD = 5
+BLOCK_STEP = 2.1
 MESH = pl.DeviceIdType.MESH
 
-KEY, VALUE = 0, 1
+KEY, VALUE, BOTH = 0, 1, 2
 OWN_Z, OWN_Y, OWN_C, F4_Z, F4_Y, F4_C, F8_Y, F8_C, F2_C, F6_C = range(10)
+CHIP_KINDS = (OWN_Z, OWN_Y, F4_Z, F4_Y, F8_Y)
 
 
 def norm_rope(block, swap, straight, crossed):
@@ -31,17 +32,31 @@
 
 
 def chunk_order(groups):
-    head = min(2, groups)
-    order = [(VALUE, g) for g in range(head)] + [(KEY, g) for g in range(head)]
-    for g in range(head, groups):
-        order += [(KEY, g), (VALUE, g)]
-    return order
+    middle = [(BOTH, g) for g in range(1, groups - 1)]
+    return [(VALUE, 0), (KEY, 0)] + middle + [(KEY, groups - 1), (VALUE, groups - 1)]
+
+
+def expected_arrivals(sizes):
+    total = len(sizes)
+    line = [("own", n) for n in range(3)] + [("far", 0)]
+    for n in range(1, total):
+        line += [("far", n)] + ([("own", n + 2)] if n + 2 < total else [])
+    at, end = 0.0, {}
+    for item in line:
+        at += sizes[item[1]]
+        end[item] = at
+    arrivals = []
+    for n, size in enumerate(sizes):
+        four, eight = end["own", n] + 2.7, end["far", n] + 2.7
+        hop = size + 3.6
+        arrivals += [(four, 4, n), (four + hop, 2, n), (eight, 8, n), (eight + hop, 6, n)]
+    return sorted(arrivals)
 
 
 def kernel(
     count, groups, copies, rows,
     q_hbm, k_hbm, v_hbm, qg_hbm, kg_hbm, freq_hbm, pos_hbm, start_hbm,
-    o_ref, win_k, win_v, hidden, q_ref, k_ref, q_rope,
+    o_ref, win, hidden, q_ref, k_ref, q_rope,
     scores_a, scores_b, top_a, top_b, weights_0, weights_1,
     qg_ref, kg_ref, freq_ref, pos_ref, start_ref,
     value_sem, in_sem, query_sem, send_sem, recv_sem,
@@ -58,15 +73,21 @@
     tiles = copies // Q_TILE
     tile_rows = Q_TILE * rows
 
-    def chunk(c, g, slot):
-        return (win_k, win_v)[c].at[g, REACH - slot]
-
-    def send(kind, c, g, source, target_slot, target):
+    order = chunk_order(groups)
+    total = len(order)
+
+    def chunk(n, slot):
+        kind, g = order[n]
+        if kind == BOTH:
+            return win.at[g, REACH - slot]
+        return win.at[g, REACH - slot, kind]
+
+    def send(kind, n, source, target_slot, target):
         return pltpu.make_async_remote_copy(
-            src_ref=chunk(c, g, source),
-            dst_ref=chunk(c, g, target_slot),
-            send_sem=send_sem.at[c, kind],
-            recv_sem=recv_sem.at[c, target_slot, g],
+            src_ref=chunk(n, source),
+            dst_ref=chunk(n, target_slot),
+            send_sem=send_sem.at[kind],
+            recv_sem=recv_sem.at[target_slot // 2 if kind in CHIP_KINDS else 0, n],
             device_id={"sp": target},
             device_id_type=MESH,
         )
@@ -87,34 +108,50 @@
         F6_C: (me >= 6, 6, 7 - 2 * core, core_peer),
     }
 
-    def start(kind, c, g):
+    def start(kind, n):
         condition, source, target_slot, target = plan[kind]
 
         @pl.when(condition)
         def _():
-            send(kind, c, g, source, target_slot, target).start()
-
-    def arrived(slot, c, g):
+            send(kind, n, source, target_slot, target).start()
+
+    def landed(ref, sem):
+        pltpu.make_async_remote_copy(
+            src_ref=ref, dst_ref=ref, send_sem=send_sem.at[0], recv_sem=sem,
+            device_id={"sp": me}, device_id_type=MESH,
+        ).wait_recv()
+
+    def own(n):
+        for kind in (OWN_Z, OWN_Y, OWN_C):
+            start(kind, n)
+
+    forwards = {4: (F4_Y, F4_C, F4_Z), 8: (F8_Y, F8_C), 2: (F2_C,), 6: (F6_C,)}
+
+    def event(slot, n):
         @pl.when(me >= slot)
         def _():
-            send(OWN_Z, c, g, 0, slot, me).wait_recv()
-
-    def own(c, g):
-        for kind in (OWN_Z, OWN_Y, OWN_C):
-            start(kind, c, g)
-
-    forwards = {4: (F4_Z, F4_Y, F4_C), 8: (F8_Y, F8_C), 2: (F2_C,), 6: (F6_C,)}
-
-    def relay(slot, c, g):
-        arrived(slot, c, g)
+            landed(chunk(n, slot), recv_sem.at[slot // 2, n])
+
         for kind in forwards[slot]:
-            start(kind, c, g)
+            start(kind, n)
+        if slot == 4 and 1 <= n < total - 2:
+            own(n + 2)
+
+    def near(kind, g, n):
+        for slots in range(1, 5):
+            first = 2 * slots - 1
+            span = win.at[g, 0:slots] if kind == BOTH else win.at[g, 0:slots, kind]
+            there = (me >= first) if slots == 4 else (me >= first) & (me < first + 2)
+
+            @pl.when(there)
+            def _():
+                landed(span, recv_sem.at[0, n])
 
     value_copies = [
         pltpu.make_async_copy(
             v_hbm.at[:, pl.ds(g * HEAD_SIZE, HEAD_SIZE)],
-            win_v.at[g, REACH],
-            value_sem.at[g],
+            win.at[g, REACH, VALUE],
+            value_sem.at[min(g, 1)],
         )
         for g in range(groups)
     ]
@@ -128,7 +165,7 @@
     width = copies * HEAD_SIZE
     query_copies = [
         pltpu.make_async_copy(
-            q_hbm.at[:, pl.ds(i * HEAD_SIZE, HEAD_SIZE)], q_ref.at[i], query_sem.at[i // copies]
+            q_hbm.at[:, pl.ds(i * HEAD_SIZE, HEAD_SIZE)], q_ref.at[i], query_sem.at[min(i // copies, 1)]
         )
         for i in range(groups * copies)
     ]
@@ -144,13 +181,10 @@
     def _():
         pl.semaphore_signal(barrier, inc=1, device_id={"sp": me - 4}, device_id_type=MESH)
 
-    for copy in value_copies[:2] + small + value_copies[2:] + query_copies:
+    for copy in value_copies[:1] + small + value_copies[1:] + query_copies:
         copy.start()
 
-    order = chunk_order(groups)
-    head = min(2, groups)
-    for copy in value_copies[:head]:
-        copy.wait()
+    value_copies[0].wait()
     inner = (me >= 4) & has_next
 
     @pl.when(inner)
@@ -161,9 +195,7 @@
     def _():
         pl.semaphore_wait(barrier, 3 if count > 4 else 2)
 
-    for n in range(head):
-        own(*order[n])
-
+    own(0)
     for copy in small:
         copy.wait()
     places = jnp.broadcast_to(pos_ref[...].astype(jnp.float32), (HEAD_SIZE, rows)).T
@@ -184,13 +216,13 @@
     straight, crossed = tables(kg_ref)
     for g in range(groups):
         rotated = norm_rope(k_ref[:, g * HEAD_SIZE:(g + 1) * HEAD_SIZE], swap, straight, crossed)
-        win_k[g, REACH] = rotated.T.astype(jnp.bfloat16)
+        win[g, REACH, KEY] = rotated.T.astype(jnp.bfloat16)
+        if g == 0:
+            rest = v_hbm.at[:, pl.ds(HEAD_SIZE, (groups - 1) * HEAD_SIZE)]
+            pltpu.make_async_copy(rest, rest, value_sem.at[1]).wait()
+            own(1)
+    own(2)
     straight, crossed = tables(qg_ref)
-
-    for copy in value_copies[head:]:
-        copy.wait()
-    for n in range(head, min(LEAD, 2 * groups)):
-        own(*order[n])
 
     starts = jnp.broadcast_to(start_ref[...], (rows, rows)).T
     token = me * rows + lax.broadcasted_iota(jnp.int32, (rows, rows), 0)
@@ -202,8 +234,7 @@
     @pl.loop(0, jnp.maximum(REACH - me, 0))
     def _(j):
         for g in range(groups):
-            win_k[g, j] = jnp.zeros((HEAD_SIZE, rows), jnp.bfloat16)
-            win_v[g, j] = jnp.zeros((rows, HEAD_SIZE), jnp.bfloat16)
+            win[g, j] = jnp.zeros((2, rows, HEAD_SIZE), jnp.bfloat16)
 
     weights_buf[tiles - 1][...] = jnp.zeros((blocks, tile_rows, rows), jnp.bfloat16)
 
@@ -215,8 +246,9 @@
     units = jnp.concatenate([unit] * Q_TILE, axis=0)
 
     def prepare(g):
-        at = pl.ds(g * width, width)
-        pltpu.make_async_copy(q_hbm.at[:, at], q_hbm.at[:, at], query_sem.at[g]).wait()
+        if g < 2:
+            some = q_hbm.at[:, pl.ds(g * width, width if g == 0 else (groups - 1) * width)]
+            pltpu.make_async_copy(some, some, query_sem.at[g]).wait()
         for head_index in range(copies):
             q_rope[g, head_index * rows:(head_index + 1) * rows] = norm_rope(
                 q_ref[g * copies + head_index], swap, straight, crossed
@@ -230,7 +262,7 @@
         for b in range(0, blocks, 2):
             pair = range(b, min(b + 2, blocks))
             keys = jnp.concatenate([
-                jnp.concatenate([win_k[g, i] for i in pair], axis=1),
+                jnp.concatenate([win[g, i, KEY] for i in pair], axis=1),
                 jnp.concatenate([hidden[i] for i in pair], axis=1),
             ], axis=0)
             part = jnp.dot(queries, keys, preferred_element_type=jnp.float32)
@@ -248,7 +280,7 @@
 
     def mix(g, tile):
         values = jnp.concatenate([
-            win_v[g].reshape(blocks * rows, HEAD_SIZE),
+            jnp.concatenate([win[g, b, VALUE] for b in range(blocks)], axis=0),
             jnp.ones((blocks * rows, HEAD_SIZE), jnp.bfloat16),
         ], axis=1)
         weights = jnp.concatenate([weights_buf[tile][b] for b in range(blocks)], axis=1)
@@ -257,99 +289,90 @@
         for r in range(Q_TILE):
             o_ref[g * copies + tile * Q_TILE + r] = mixed[r * rows:(r + 1) * rows].astype(jnp.bfloat16)
 
-    total = 2 * groups
-    first_step = 16.8
-
-    def arrival(slot, n):
-        four = n + 3.4 if n < LEAD else 2 * n - LEAD + 4.4
-        eight = min(2 * n + LEAD + 3.4, 2 * total + 2.4 - (total - 1 - n))
-        return {4: four, 2: four + 2.9, 8: eight, 6: eight + 3.0}[slot]
-
-    early = sorted(
-        (arrival(slot, n), slot, n) for slot in (4, 2, 8, 6) for n in range(total)
-    )
-    late = [event for event in early if event[0] >= first_step]
-    early = [event for event in early if event[0] < first_step]
-
-    def event(slot, n):
-        relay(slot, *order[n])
-        if slot == 4 and n + LEAD < total:
-            own(*order[n + LEAD])
-
-    for g in range(min(2, groups)):
+    arrivals = expected_arrivals([2 if kind == BOTH else 1 for kind, _ in order])
+    first_tile = [when for when, slot, n in arrivals if (slot, n) == (6, 1)][0] + 0.1
+    early = [(slot, n) for when, slot, n in arrivals if when < first_tile]
+    by_block, tail = {}, []
+    block = 2 * (groups - 1)
+    for when, slot, n in reversed(arrivals):
+        if when >= first_tile:
+            at = max(int((when - first_tile - 1.5) / BLOCK_STEP), 0)
+            block = min(block, at, max(2 * n - 3, 0) if n < total - 2 else at)
+            if block < 2 * (groups - 1):
+                by_block.setdefault(block, []).insert(0, (slot, n))
+            else:
+                tail.insert(0, (slot, n))
+
+    ready = min(3, groups)
+    for g in range(ready):
         prepare(g)
-    ready = min(2, groups)
-    for at, (_, slot, n) in enumerate(early):
+    for slot, n in early:
         event(slot, n)
-        if at % 2 == 1 and ready < groups:
+        if ready < groups:
             prepare(ready)
             ready += 1
     for g in range(ready, groups):
         prepare(g)
 
-    by_tile = {}
-    for when, slot, n in late:
-        step = max(0, min(int((when - first_step) * tiles / 4), groups * tiles - 1))
-        by_tile.setdefault(step, []).append((slot, n))
-
-    def near(c, g):
-        for slot in (1, 3, 5, 7):
-            arrived(slot, c, g)
-
-    near(VALUE, 0)
-    near(KEY, 0)
+    def relays(g, tile):
+        for block, todo in by_block.items():
+            if block % 2 != tile:
+                continue
+            if isinstance(g, int):
+                if g == block // 2:
+                    for slot, n in todo:
+                        event(slot, n)
+            elif block // 2 < groups - 2:
+                @pl.when(g == block // 2)
+                def _():
+                    for slot, n in todo:
+                        event(slot, n)
+
+    near(VALUE, 0, 0)
+    near(KEY, 0, 1)
     score(0, 0)
 
-    def relays(g, tile):
-        for (kind_step, todo) in by_tile.items():
-            if kind_step % tiles != tile:
-                continue
-
-            @pl.when(g == kind_step // tiles)
-            def _():
-                for slot, n in todo:
-                    event(slot, n)
-
-    @pl.loop(0, groups - 1)
+    last = groups - 1
+
+    @pl.loop(0, last - 1)
     def _(g):
-        for tile in range(tiles):
-            relays(g, tile)
-            if tile == 1:
-                @pl.when(g > 0)
-                def _():
-                    near(VALUE, g)
-            if tile == tiles - 1:
-                near(KEY, g + 1)
-                score(g + 1, 0)
-            else:
-                score(g, tile + 1)
-            soften(tile)
-            if tile == 0:
-                mix(jnp.maximum(g - 1, 0), tiles - 1)
-            else:
-                mix(g, tile - 1)
-
-    last = groups - 1
+        relays(g, 0)
+        score(g, 1)
+        soften(0)
+        mix(jnp.maximum(g - 1, 0), 1)
+        relays(g, 1)
+        near(BOTH, g + 1, g + 2)
+        score(g + 1, 0)
+        soften(1)
+        mix(g, 0)
+
+    relays(last - 1, 0)
+    score(last - 1, 1)
+    soften(0)
+    mix(last - 2, 1)
+    relays(last - 1, 1)
+    soften(1)
+    mix(last - 1, 0)
+    for slot, n in tail:
+        event(slot, n)
+    mix(last - 1, 1)
+    near(KEY, last, total - 2)
     for tile in range(tiles):
-        relays(last, tile)
-        if tile < tiles - 1:
-            score(last, tile + 1)
+        score(last, tile)
+    for tile in range(tiles):
         soften(tile)
-        if tile == 0:
-            mix(max(last - 1, 0), tiles - 1)
-    near(VALUE, last)
+    near(VALUE, last, total - 1)
     for tile in range(tiles):
         mix(last, tile)
 
-    for c in (KEY, VALUE):
-        whole = (win_k, win_v)[c].at[:, REACH]
-        for kind, (condition, _, _, target) in plan.items():
-            @pl.when(condition)
-            def _():
-                pltpu.make_async_remote_copy(
-                    src_ref=whole, dst_ref=whole, send_sem=send_sem.at[c, kind],
-                    recv_sem=recv_sem.at[c, 0, 0], device_id={"sp": target}, device_id_type=MESH,
-                ).wait_send()
+    whole = win.at[:, REACH]
+    for kind, (condition, _, _, target) in plan.items():
+        @pl.when(condition)
+        def _():
+            pltpu.make_async_remote_copy(
+                src_ref=whole, dst_ref=whole, send_sem=send_sem.at[kind],
+                recv_sem=recv_sem.at[0, 0], device_id={"sp": target}, device_id_type=MESH,
+            ).wait_send()
 
 
 def leave(heads_ref, o_hbm, sem):
@@ -367,6 +390,7 @@
         groups = key_projection.shape[1] // HEAD_SIZE
         copies = query_proj.shape[1] // key_projection.shape[1]
         assert rows * REACH >= DOC_MAX and count % 4 == 0
+        assert rows == HEAD_SIZE and groups >= 4 and copies == 2 * Q_TILE
         half_dim = HEAD_SIZE // 2
         inv_freq = ROPE_BASE ** (-(np.arange(half_dim) * 2.0 / HEAD_SIZE))
         freq = jnp.asarray(np.concatenate([inv_freq, inv_freq])[None, :], jnp.float32)
@@ -378,8 +402,7 @@
             in_specs=[pl.BlockSpec(memory_space=pl.ANY)] * 8,
             out_specs=pl.BlockSpec(memory_space=pltpu.VMEM),
             scratch_shapes=[
-                pltpu.VMEM((groups, blocks, HEAD_SIZE, rows), jnp.bfloat16),
-                pltpu.VMEM((groups, blocks, rows, HEAD_SIZE), jnp.bfloat16),
+                pltpu.VMEM((groups, blocks, 2, rows, HEAD_SIZE), jnp.bfloat16),
                 pltpu.VMEM((blocks, rows, rows), jnp.bfloat16),
                 pltpu.VMEM((groups * copies, rows, HEAD_SIZE), jnp.bfloat16),
                 pltpu.VMEM(key_projection.shape, jnp.bfloat16),
@@ -395,11 +418,11 @@
                 pltpu.VMEM((1, HEAD_SIZE), jnp.float32),
                 pltpu.VMEM((1, rows), jnp.int32),
                 pltpu.VMEM((1, rows), jnp.int32),
-                pltpu.SemaphoreType.DMA((groups,)),
+                pltpu.SemaphoreType.DMA((2,)),
                 pltpu.SemaphoreType.DMA((6,)),
-                pltpu.SemaphoreType.DMA((groups,)),
-                pltpu.SemaphoreType.DMA((2, 10)),
-                pltpu.SemaphoreType.DMA((2, REACH + 1, groups)),
+                pltpu.SemaphoreType.DMA((2,)),
+                pltpu.SemaphoreType.DMA((10,)),
+                pltpu.SemaphoreType.DMA((5, groups + 2)),
             ],
             compiler_params=pltpu.CompilerParams(
                 collective_id=0, has_side_effects=True, vmem_limit_bytes=41943040

time: 40 us -> 40.7 us (1.018)
  Pallas kernels: 39.8 us -> 40.5 us
    pallas_call x1, Pallas kernels: 38.5 us -> 39.2 us  [body(): pl.pallas_call(functools.partial(kernel, count, groups, copies, rows), ou...]
where the time goes in v4:
time: 40.7 us; the launch traced here: 40.5 us
  Pallas kernels  40.5 us (100%)
    pallas_call x1, Pallas kernels, body(): pl.pallas_call(functools.partial(kernel, count, groups, copies, rows), ou...  39.2 us
    pallas_call x1, Pallas kernels, body(): pl.pallas_call(leave, out_shape=jax.ShapeDtypeStruct(query_proj.shape, jn...  1.29 us

profile of v4, /device:TPU:16, one launch (start us, length us, event | category | flops | bytes accessed | tf_op | source)
XLA Modules:
  0.0 40.5 jit_solution(3281939615566107149)
XLA Ops:
  0.0 39.2 %shard_map.82.heads_ref = bf16[64,128,128]{2,1,0:T(8,128)(2,1)S(1)} custom-call(bf16[128,8192]{1,0:T(8,128)(2,1)} %q_hbm.1, bf16[128,1024]{1,0:T(8,128)(2,1)} %k_hbm.1, bf16[128,1024]{1,0:T(8,128)(2,1)} %v_hbm.1, f32[1,128]{1,0:T(1,128)} %bitcast.4, f32[1,128]{1,0:T(1,128)} %bitcast.5, f32[1,128]{1,0:T(1,128)} %constant.2.clone.freq_hbm, s32[1,128]{1,0:T(1,128)} %bitcast.6, ...), custom_call_target="tpu_custom_call" | custom-call | tf_op jit(solution)/shard_map/pallas_call | solution.py:399
  39.2 1.3 %shard_map.83 = bf16[128,8192]{1,0:T(8,128)(2,1)} custom-call(bf16[64,128,128]{2,1,0:T(8,128)(2,1)S(1)} %shard_map.82.heads_ref), custom_call_target="tpu_custom_call" | custom-call | tf_op jit(solution)/shard_map/pallas_call | solution.py:436

commit v5 on v4

--- a/solution.py
+++ b/solution.py
@@ -15,8 +15,13 @@
 ROPE_BASE = 1000000.0
 NORM_EPS = 1e-06
 HIDDEN = -1e30
-Q_TILE = 4
-BLOCK_STEP = 2.1
+Q_TILE = 1
+AHEAD = 2
+NEAR_TIME = 2.0
+FAR_TIME = 1.5
+CORE_HOP = 1.6
+PATIENCE = 0.5
+EARLIER = 1
 MESH = pl.DeviceIdType.MESH
 
 KEY, VALUE, BOTH = 0, 1, 2
@@ -46,18 +51,19 @@
         at += sizes[item[1]]
         end[item] = at
     arrivals = []
-    for n, size in enumerate(sizes):
-        four, eight = end["own", n] + 2.7, end["far", n] + 2.7
-        hop = size + 3.6
-        arrivals += [(four, 4, n), (four + hop, 2, n), (eight, 8, n), (eight + hop, 6, n)]
+    for n in range(total):
+        arrivals += [(end["own", n] + 2.7, 4, n), (end["far", n] + 2.7, 8, n)]
+    free = 0.0
+    for when, slot, n in sorted(arrivals):
+        free = max(free, when) + sizes[n]
+        arrivals.append((free + 3.7, slot - 2, n))
     return sorted(arrivals)
 
 
 def kernel(
     count, groups, copies, rows,
     q_hbm, k_hbm, v_hbm, qg_hbm, kg_hbm, freq_hbm, pos_hbm, start_hbm,
-    o_ref, win, hidden, q_ref, k_ref, q_rope,
-    scores_a, scores_b, top_a, top_b, weights_0, weights_1,
+    o_ref, win, hidden, q_ref, k_ref, q_rope, sums, tops,
     qg_ref, kg_ref, freq_ref, pos_ref, start_ref,
     value_sem, in_sem, query_sem, send_sem, recv_sem,
 ):
@@ -67,9 +73,6 @@
     core_peer = me + 1 - 2 * core
     side_peer = me + 2 - 4 * side
     blocks = REACH + 1
-    scores_buf = [scores_a, scores_b]
-    top_buf = [top_a, top_b]
-    weights_buf = [weights_0, weights_1]
     tiles = copies // Q_TILE
     tile_rows = Q_TILE * rows
 
@@ -82,12 +85,17 @@
             return win.at[g, REACH - slot]
         return win.at[g, REACH - slot, kind]
 
+    def semaphore_of(kind, target_slot):
+        if kind in CHIP_KINDS:
+            return target_slot // 2
+        return 0 if kind in (OWN_C, F2_C) else 5 if kind in (F6_C, F8_C) else (5 - 5 * core)
+
     def send(kind, n, source, target_slot, target):
         return pltpu.make_async_remote_copy(
             src_ref=chunk(n, source),
             dst_ref=chunk(n, target_slot),
             send_sem=send_sem.at[kind],
-            recv_sem=recv_sem.at[target_slot // 2 if kind in CHIP_KINDS else 0, n],
+            recv_sem=recv_sem.at[semaphore_of(kind, target_slot), n],
             device_id={"sp": target},
             device_id_type=MESH,
         )
@@ -137,15 +145,14 @@
         if slot == 4 and 1 <= n < total - 2:
             own(n + 2)
 
-    def near(kind, g, n):
-        for slots in range(1, 5):
-            first = 2 * slots - 1
+    def from_peer(far, kind, g, n):
+        least, sem = (5, 5) if far else (1, 0)
+        for slots, there in ((1, (me >= least) & (me < least + 2)), (2, me >= least + 2)):
             span = win.at[g, 0:slots] if kind == BOTH else win.at[g, 0:slots, kind]
-            there = (me >= first) if slots == 4 else (me >= first) & (me < first + 2)
 
             @pl.when(there)
             def _():
-                landed(span, recv_sem.at[0, n])
+                landed(span, recv_sem.at[sem, n])
 
     value_copies = [
         pltpu.make_async_copy(
@@ -236,8 +243,6 @@
         for g in range(groups):
             win[g, j] = jnp.zeros((2, rows, HEAD_SIZE), jnp.bfloat16)
 
-    weights_buf[tiles - 1][...] = jnp.zeros((blocks, tile_rows, rows), jnp.bfloat16)
-
     scale = HEAD_SIZE ** (-0.5) * math.log2(math.e)
     unit = (
         lax.broadcasted_iota(jnp.int32, (rows, rows), 0)
@@ -254,54 +259,69 @@
                 q_ref[g * copies + head_index], swap, straight, crossed
             ).astype(jnp.bfloat16)
 
-    def score(g, tile):
-        queries = jnp.concatenate(
-            [q_rope[g, tile * tile_rows:(tile + 1) * tile_rows], units], axis=1
-        )
-        best = None
-        for b in range(0, blocks, 2):
-            pair = range(b, min(b + 2, blocks))
-            keys = jnp.concatenate([
-                jnp.concatenate([win[g, i, KEY] for i in pair], axis=1),
-                jnp.concatenate([hidden[i] for i in pair], axis=1),
-            ], axis=0)
-            part = jnp.dot(queries, keys, preferred_element_type=jnp.float32)
-            for at, i in enumerate(pair):
-                piece = part[:, at * rows:(at + 1) * rows]
-                scores_buf[tile % 2][i] = piece
-                best = piece if best is None else jnp.maximum(best, piece)
-        top_buf[tile % 2][...] = best
-
-    def soften(tile):
-        top = jnp.max(top_buf[tile % 2][...], axis=1, keepdims=True)
-        for b in range(blocks):
-            part = scores_buf[tile % 2][b]
-            weights_buf[tile][b] = jnp.exp2((part - top) * scale).astype(jnp.bfloat16)
-
-    def mix(g, tile):
+    def operands(g, chosen):
+        keys = jnp.concatenate([
+            jnp.concatenate([win[g, b, KEY] for b in chosen], axis=1),
+            jnp.concatenate([hidden[b] for b in chosen], axis=1),
+        ], axis=0)
         values = jnp.concatenate([
-            jnp.concatenate([win[g, b, VALUE] for b in range(blocks)], axis=0),
-            jnp.ones((blocks * rows, HEAD_SIZE), jnp.bfloat16),
+            jnp.concatenate([win[g, b, VALUE] for b in chosen], axis=0),
+            jnp.ones((len(chosen) * rows, HEAD_SIZE), jnp.bfloat16),
         ], axis=1)
-        weights = jnp.concatenate([weights_buf[tile][b] for b in range(blocks)], axis=1)
-        mixed = jnp.dot(weights, values, preferred_element_type=jnp.float32)
-        mixed = mixed[:, :HEAD_SIZE] / mixed[:, HEAD_SIZE:]
-        for r in range(Q_TILE):
-            o_ref[g * copies + tile * Q_TILE + r] = mixed[r * rows:(r + 1) * rows].astype(jnp.bfloat16)
+        return keys, values
+
+    def queries_of(g, tile):
+        return jnp.concatenate([q_rope[g, tile * tile_rows:(tile + 1) * tile_rows], units], axis=1)
+
+    far_blocks = range(0, REACH // 2)
+    near_blocks = range(REACH // 2, blocks)
+
+    def attend_near(g):
+        keys, values = operands(g, near_blocks)
+        for tile in range(tiles):
+            scores = jnp.dot(queries_of(g, tile), keys, preferred_element_type=jnp.float32)
+            top = jnp.max(scores, axis=1, keepdims=True)
+            weights = jnp.exp2((scores - top) * scale).astype(jnp.bfloat16)
+            sums[g, tile] = jnp.dot(weights, values, preferred_element_type=jnp.float32)
+            tops[g, tile] = jnp.broadcast_to(top, (tile_rows, HEAD_SIZE))
+
+    def attend_far(g):
+        keys, values = operands(g, far_blocks)
+        for tile in range(tiles):
+            scores = jnp.dot(queries_of(g, tile), keys, preferred_element_type=jnp.float32)
+            near_top = tops[g, tile]
+            top = jnp.maximum(near_top, jnp.max(scores, axis=1, keepdims=True))
+            wide = jnp.concatenate([top] * len(far_blocks), axis=1)
+            weights = jnp.exp2((scores - wide) * scale).astype(jnp.bfloat16)
+            factor = jnp.exp2((near_top - top) * scale)
+            mixed = jnp.dot(weights, values, preferred_element_type=jnp.float32)
+            mixed = sums[g, tile] * jnp.concatenate([factor, factor], axis=1) + mixed
+            mixed = mixed[:, :HEAD_SIZE] / mixed[:, HEAD_SIZE:]
+            for r in range(Q_TILE):
+                o_ref[g * copies + tile * Q_TILE + r] = mixed[r * rows:(r + 1) * rows].astype(jnp.bfloat16)
 
     arrivals = expected_arrivals([2 if kind == BOTH else 1 for kind, _ in order])
-    first_tile = [when for when, slot, n in arrivals if (slot, n) == (6, 1)][0] + 0.1
-    early = [(slot, n) for when, slot, n in arrivals if when < first_tile]
-    by_block, tail = {}, []
-    block = 2 * (groups - 1)
+    last = groups - 1
+    plan_of_blocks = [("near", g) for g in range(AHEAD)]
+    for g in range(groups):
+        plan_of_blocks += [("far", g)] + ([("near", g + AHEAD)] if g + AHEAD < groups else [])
+    pieces = [[n for n in range(total) if order[n][1] == g] for g in range(groups)]
+    when_of = {(slot, n): when for when, slot, n in arrivals}
+    clock, starts_at = 0.0, []
+    for what, g in plan_of_blocks:
+        slot = 6 if what == "far" else 2
+        clock = max([clock] + [when_of[slot, n] + CORE_HOP for n in pieces[g]])
+        starts_at.append(clock)
+        clock += FAR_TIME if what == "far" else NEAR_TIME
+    reader = {(what, g): i for i, (what, g) in enumerate(plan_of_blocks)}
+    by_block = {}
+    block = len(plan_of_blocks) - 1
     for when, slot, n in reversed(arrivals):
-        if when >= first_tile:
-            at = max(int((when - first_tile - 1.5) / BLOCK_STEP), 0)
-            block = min(block, at, max(2 * n - 3, 0) if n < total - 2 else at)
-            if block < 2 * (groups - 1):
-                by_block.setdefault(block, []).insert(0, (slot, n))
-            else:
-                tail.insert(0, (slot, n))
+        at = [i for i, begin in enumerate(starts_at) if begin > when - PATIENCE]
+        read = reader["far" if slot in (6, 8) else "near", order[n][1]]
+        block = min([block, max(read - EARLIER, 0) if read < len(plan_of_blocks) - 1 else read] + at[:1])
+        by_block.setdefault(block, []).insert(0, (slot, n))
+    early = by_block.pop(0)
 
     ready = min(3, groups)
     for g in range(ready):
@@ -314,56 +334,57 @@
     for g in range(ready, groups):
         prepare(g)
 
-    def relays(g, tile):
-        for block, todo in by_block.items():
-            if block % 2 != tile:
-                continue
-            if isinstance(g, int):
-                if g == block // 2:
-                    for slot, n in todo:
-                        event(slot, n)
-            elif block // 2 < groups - 2:
-                @pl.when(g == block // 2)
+    def relays(block):
+        for slot, n in by_block.get(block, []):
+            event(slot, n)
+
+    def relays_in_loop(g, first):
+        for at in range(groups - AHEAD):
+            if first + 2 * at in by_block:
+                @pl.when(g == at)
                 def _():
-                    for slot, n in todo:
-                        event(slot, n)
-
-    near(VALUE, 0, 0)
-    near(KEY, 0, 1)
-    score(0, 0)
-
-    last = groups - 1
-
-    @pl.loop(0, last - 1)
+                    relays(first + 2 * at)
+
+    def await_pieces(far, g):
+        for n in pieces[g]:
+            from_peer(far, order[n][0], g, n)
+
+    for g in range(AHEAD):
+        if g:
+            relays(g)
+        await_pieces(False, g)
+        attend_near(g)
+
+    @pl.loop(0, groups - AHEAD)
     def _(g):
-        relays(g, 0)
-        score(g, 1)
-        soften(0)
-        mix(jnp.maximum(g - 1, 0), 1)
-        relays(g, 1)
-        near(BOTH, g + 1, g + 2)
-        score(g + 1, 0)
-        soften(1)
-        mix(g, 0)
-
-    relays(last - 1, 0)
-    score(last - 1, 1)
-    soften(0)
-    mix(last - 2, 1)
-    relays(last - 1, 1)
-    soften(1)
-    mix(last - 1, 0)
-    for slot, n in tail:
-        event(slot, n)
-    mix(last - 1, 1)
-    near(KEY, last, total - 2)
-    for tile in range(tiles):
-        score(last, tile)
-    for tile in range(tiles):
-        soften(tile)
-    near(VALUE, last, total - 1)
-    for tile in range(tiles):
-        mix(last, tile)
+        relays_in_loop(g, AHEAD)
+
+        @pl.when(g == 0)
+        def _():
+            await_pieces(True, 0)
+
+        @pl.when(g > 0)
+        def _():
+            from_peer(True, BOTH, jnp.maximum(g, 1), jnp.maximum(g, 1) + 1)
+
+        attend_far(g)
+        relays_in_loop(g, AHEAD + 1)
+
+        @pl.when(g + AHEAD < last)
+        def _():
+            other = jnp.minimum(g + AHEAD, last - 1)
+            from_peer(False, BOTH, other, other + 1)
+
+        @pl.when(g + AHEAD == last)
+        def _():
+            await_pieces(False, last)
+
+        attend_near(g + AHEAD)
+
+    for g in range(groups - AHEAD, groups):
+        relays(reader["far", g])
+        await_pieces(True, g)
+        attend_far(g)
 
     whole = win.at[:, REACH]
     for kind, (condition, _, _, target) in plan.items():
@@ -390,12 +411,11 @@
         groups = key_projection.shape[1] // HEAD_SIZE
         copies = query_proj.shape[1] // key_projection.shape[1]
         assert rows * REACH >= DOC_MAX and count % 4 == 0
-        assert rows == HEAD_SIZE and groups >= 4 and copies == 2 * Q_TILE
+        assert rows == HEAD_SIZE and groups >= 4 and copies % Q_TILE == 0
         half_dim = HEAD_SIZE // 2
         inv_freq = ROPE_BASE ** (-(np.arange(half_dim) * 2.0 / HEAD_SIZE))
         freq = jnp.asarray(np.concatenate([inv_freq, inv_freq])[None, :], jnp.float32)
         blocks = REACH + 1
-        tile_rows = Q_TILE * rows
         heads = pl.pallas_call(
             functools.partial(kernel, count, groups, copies, rows),
             out_shape=jax.ShapeDtypeStruct((groups * copies, rows, HEAD_SIZE), jnp.bfloat16),
@@ -407,12 +427,8 @@
                 pltpu.VMEM((groups * copies, rows, HEAD_SIZE), jnp.bfloat16),
                 pltpu.VMEM(key_projection.shape, jnp.bfloat16),
                 pltpu.VMEM((groups, copies * rows, HEAD_SIZE), jnp.bfloat16),
-                pltpu.VMEM((blocks, tile_rows, rows), jnp.float32),
-                pltpu.VMEM((blocks, tile_rows, rows), jnp.float32),
-                pltpu.VMEM((tile_rows, rows), jnp.float32),
-                pltpu.VMEM((tile_rows, rows), jnp.float32),
-                pltpu.VMEM((blocks, tile_rows, rows), jnp.bfloat16),
-                pltpu.VMEM((blocks, tile_rows, rows), jnp.bfloat16),
+                pltpu.VMEM((groups, copies // Q_TILE, Q_TILE * rows, 2 * HEAD_SIZE), jnp.float32),
+                pltpu.VMEM((groups, copies // Q_TILE, Q_TILE * rows, HEAD_SIZE), jnp.float32),
                 pltpu.VMEM((1, HEAD_SIZE), jnp.float32),
                 pltpu.VMEM((1, HEAD_SIZE), jnp.float32),
                 pltpu.VMEM((1, HEAD_SIZE), jnp.float32),
@@ -422,7 +438,7 @@
                 pltpu.SemaphoreType.DMA((6,)),
                 pltpu.SemaphoreType.DMA((2,)),
                 pltpu.SemaphoreType.DMA((10,)),
-                pltpu.SemaphoreType.DMA((5, groups + 2)),
+                pltpu.SemaphoreType.DMA((6, groups + 2)),
             ],
             compiler_params=pltpu.CompilerParams(
                 collective_id=0, has_side_effects=True, vmem_limit_bytes=41943040

time: 40.7 us -> 36.2 us (0.89)
  the two profiles are of different devices: /device:TPU:16 before, /device:TPU:24 now
where the time goes in v5:
time: 36.2 us; the launch traced here: 36.1 us
  Pallas kernels  36 us (99%)
    pallas_call x1, Pallas kernels, body(): pl.pallas_call(functools.partial(kernel, count, groups, copies, rows), ou...  34.8 us
    pallas_call x1, Pallas kernels, body(): pl.pallas_call(leave, out_shape=jax.ShapeDtypeStruct(query_proj.shape, jn...  1.29 us

profile of v5, /device:TPU:24, one launch (start us, length us, event | category | flops | bytes accessed | tf_op | source)
XLA Modules:
  0.0 36.1 jit_solution(14357508418489094491)
XLA Ops:
  0.0 34.8 %shard_map.82.heads_ref = bf16[64,128,128]{2,1,0:T(8,128)(2,1)S(1)} custom-call(bf16[128,8192]{1,0:T(8,128)(2,1)} %q_hbm.1, bf16[128,1024]{1,0:T(8,128)(2,1)} %k_hbm.1, bf16[128,1024]{1,0:T(8,128)(2,1)} %v_hbm.1, f32[1,128]{1,0:T(1,128)} %bitcast.4, f32[1,128]{1,0:T(1,128)} %bitcast.5, f32[1,128]{1,0:T(1,128)} %constant.2.clone.freq_hbm, s32[1,128]{1,0:T(1,128)} %bitcast.6, ...), custom_call_target="tpu_custom_call" | custom-call | tf_op jit(solution)/shard_map/pallas_call | solution.py:419
  34.8 1.3 %shard_map.83 = bf16[128,8192]{1,0:T(8,128)(2,1)} custom-call(bf16[64,128,128]{2,1,0:T(8,128)(2,1)S(1)} %shard_map.82.heads_ref), custom_call_target="tpu_custom_call" | custom-call | tf_op jit(solution)/shard_map/pallas_call | solution.py:452

commit v6 on v5

--- a/solution.py
+++ b/solution.py
@@ -41,11 +41,19 @@
     return [(VALUE, 0), (KEY, 0)] + middle + [(KEY, groups - 1), (VALUE, groups - 1)]
 
 
+def released(total, n):
+    if n < 1 or n > total - 4:
+        return []
+    if n == total - 4:
+        return [total - 1]
+    return [n + 2] if n < total - 5 else [n + 2, n + 3]
+
+
 def expected_arrivals(sizes):
     total = len(sizes)
     line = [("own", n) for n in range(3)] + [("far", 0)]
     for n in range(1, total):
-        line += [("far", n)] + ([("own", n + 2)] if n + 2 < total else [])
+        line += [("far", n)] + [("own", m) for m in released(total, n)]
     at, end = 0.0, {}
     for item in line:
         at += sizes[item[1]]
@@ -142,8 +150,8 @@
 
         for kind in forwards[slot]:
             start(kind, n)
-        if slot == 4 and 1 <= n < total - 2:
-            own(n + 2)
+        for m in released(total, n) if slot == 4 else ():
+            own(m)
 
     def from_peer(far, kind, g, n):
         least, sem = (5, 5) if far else (1, 0)
@@ -188,7 +196,7 @@
     def _():
         pl.semaphore_signal(barrier, inc=1, device_id={"sp": me - 4}, device_id_type=MESH)
 
-    for copy in value_copies[:1] + small + value_copies[1:] + query_copies:
+    for copy in value_copies[:1] + small + value_copies[1:]:
         copy.start()
 
     value_copies[0].wait()
@@ -203,6 +211,8 @@
         pl.semaphore_wait(barrier, 3 if count > 4 else 2)
 
     own(0)
+    for copy in query_copies:
+        copy.start()
     for copy in small:
         copy.wait()
     places = jnp.broadcast_to(pos_ref[...].astype(jnp.float32), (HEAD_SIZE, rows)).T
@@ -411,7 +421,7 @@
         groups = key_projection.shape[1] // HEAD_SIZE
         copies = query_proj.shape[1] // key_projection.shape[1]
         assert rows * REACH >= DOC_MAX and count % 4 == 0
-        assert rows == HEAD_SIZE and groups >= 4 and copies % Q_TILE == 0
+        assert rows == HEAD_SIZE and groups >= 6 and copies % Q_TILE == 0
         half_dim = HEAD_SIZE // 2
         inv_freq = ROPE_BASE ** (-(np.arange(half_dim) * 2.0 / HEAD_SIZE))
         freq = jnp.asarray(np.concatenate([inv_freq, inv_freq])[None, :], jnp.float32)

time: 36.2 us -> 35.3 us (0.975)
  the two profiles are of different devices: /device:TPU:24 before, /device:TPU:16 now
where the time goes in v6:
time: 35.3 us; the launch traced here: 34.7 us
  Pallas kernels  34.6 us (98%)
    pallas_call x1, Pallas kernels, body(): pl.pallas_call(functools.partial(kernel, count, groups, copies, rows), ou...  33.4 us
    pallas_call x1, Pallas kernels, body(): pl.pallas_call(leave, out_shape=jax.ShapeDtypeStruct(query_proj.shape, jn...  1.29 us

profile of v6, /device:TPU:16, one launch (start us, length us, event | category | flops | bytes accessed | tf_op | source)
XLA Modules:
  0.0 34.7 jit_solution(3861190568975775324)
XLA Ops:
  0.0 33.4 %shard_map.82.heads_ref = bf16[64,128,128]{2,1,0:T(8,128)(2,1)S(1)} custom-call(bf16[128,8192]{1,0:T(8,128)(2,1)} %q_hbm.1, bf16[128,1024]{1,0:T(8,128)(2,1)} %k_hbm.1, bf16[128,1024]{1,0:T(8,128)(2,1)} %v_hbm.1, f32[1,128]{1,0:T(1,128)} %bitcast.4, f32[1,128]{1,0:T(1,128)} %bitcast.5, f32[1,128]{1,0:T(1,128)} %constant.2.clone.freq_hbm, s32[1,128]{1,0:T(1,128)} %bitcast.6, ...), custom_call_target="tpu_custom_call" | custom-call | tf_op jit(solution)/shard_map/pallas_call | solution.py:429
  33.4 1.3 %shard_map.83 = bf16[128,8192]{1,0:T(8,128)(2,1)} custom-call(bf16[64,128,128]{2,1,0:T(8,128)(2,1)S(1)} %shard_map.82.heads_ref), custom_call_target="tpu_custom_call" | custom-call | tf_op jit(solution)/shard_map/pallas_call | solution.py:462

commit v7 on v6

--- a/solution.py
+++ b/solution.py
@@ -68,10 +68,66 @@
     return sorted(arrivals)
 
 
+SCALE = HEAD_SIZE ** (-0.5) * math.log2(math.e)
+
+
+def unit_rows(rows):
+    unit = (
+        lax.broadcasted_iota(jnp.int32, (rows, rows), 0)
+        == lax.broadcasted_iota(jnp.int32, (rows, rows), 1)
+    ).astype(jnp.bfloat16)
+    return jnp.concatenate([unit] * Q_TILE, axis=0)
+
+
+def operands(win, hidden, g, chosen):
+    rows = win.shape[3]
+    keys = jnp.concatenate([
+        jnp.concatenate([win[g, b, KEY] for b in chosen], axis=1),
+        jnp.concatenate([hidden[b] for b in chosen], axis=1),
+    ], axis=0)
+    values = jnp.concatenate([
+        jnp.concatenate([win[g, b, VALUE] for b in chosen], axis=0),
+        jnp.ones((len(chosen) * rows, HEAD_SIZE), jnp.bfloat16),
+    ], axis=1)
+    return keys, values
+
+
+def queries_of(q_rope, units, g, tile):
+    size = units.shape[0]
+    return jnp.concatenate([q_rope[g, tile * size:(tile + 1) * size], units], axis=1)
+
+
+def attend_near(win, hidden, q_rope, sums, tops, units, g):
+    keys, values = operands(win, hidden, g, range(REACH // 2, REACH + 1))
+    for tile in range(sums.shape[1]):
+        scores = jnp.dot(queries_of(q_rope, units, g, tile), keys, preferred_element_type=jnp.float32)
+        top = jnp.max(scores, axis=1, keepdims=True)
+        weights = jnp.exp2((scores - top) * SCALE).astype(jnp.bfloat16)
+        sums[g, tile] = jnp.dot(weights, values, preferred_element_type=jnp.float32)
+        tops[g, tile] = jnp.broadcast_to(top, tops.shape[2:])
+
+
+def attend_far(win, hidden, q_rope, sums, tops, units, g, o_ref, first):
+    rows = win.shape[3]
+    keys, values = operands(win, hidden, g, range(REACH // 2))
+    for tile in range(sums.shape[1]):
+        scores = jnp.dot(queries_of(q_rope, units, g, tile), keys, preferred_element_type=jnp.float32)
+        near_top = tops[g, tile]
+        top = jnp.maximum(near_top, jnp.max(scores, axis=1, keepdims=True))
+        wide = jnp.concatenate([top] * (REACH // 2), axis=1)
+        weights = jnp.exp2((scores - wide) * SCALE).astype(jnp.bfloat16)
+        factor = jnp.exp2((near_top - top) * SCALE)
+        mixed = jnp.dot(weights, values, preferred_element_type=jnp.float32)
+        mixed = sums[g, tile] * jnp.concatenate([factor, factor], axis=1) + mixed
+        mixed = mixed[:, :HEAD_SIZE] / mixed[:, HEAD_SIZE:]
+        for r in range(Q_TILE):
+            o_ref[first + tile * Q_TILE + r] = mixed[r * rows:(r + 1) * rows].astype(jnp.bfloat16)
+
+
 def kernel(
     count, groups, copies, rows,
     q_hbm, k_hbm, v_hbm, qg_hbm, kg_hbm, freq_hbm, pos_hbm, start_hbm,
-    o_ref, win, hidden, q_ref, k_ref, q_rope, sums, tops,
+    o_ref, win, hidden, q_rope, sums, tops, q_ref, k_ref,
     qg_ref, kg_ref, freq_ref, pos_ref, start_ref,
     value_sem, in_sem, query_sem, send_sem, recv_sem,
 ):
@@ -81,8 +137,6 @@
     core_peer = me + 1 - 2 * core
     side_peer = me + 2 - 4 * side
     blocks = REACH + 1
-    tiles = copies // Q_TILE
-    tile_rows = Q_TILE * rows
 
     order = chunk_order(groups)
     total = len(order)
@@ -253,12 +307,7 @@
         for g in range(groups):
             win[g, j] = jnp.zeros((2, rows, HEAD_SIZE), jnp.bfloat16)
 
-    scale = HEAD_SIZE ** (-0.5) * math.log2(math.e)
-    unit = (
-        lax.broadcasted_iota(jnp.int32, (rows, rows), 0)
-        == lax.broadcasted_iota(jnp.int32, (rows, rows), 1)
-    ).astype(jnp.bfloat16)
-    units = jnp.concatenate([unit] * Q_TILE, axis=0)
+    units = unit_rows(rows)
 
     def prepare(g):
         if g < 2:
@@ -269,46 +318,11 @@
                 q_ref[g * copies + head_index], swap, straight, crossed
             ).astype(jnp.bfloat16)
 
-    def operands(g, chosen):
-        keys = jnp.concatenate([
-            jnp.concatenate([win[g, b, KEY] for b in chosen], axis=1),
-            jnp.concatenate([hidden[b] for b in chosen], axis=1),
-        ], axis=0)
-        values = jnp.concatenate([
-            jnp.concatenate([win[g, b, VALUE] for b in chosen], axis=0),
-            jnp.ones((len(chosen) * rows, HEAD_SIZE), jnp.bfloat16),
-        ], axis=1)
-        return keys, values
-
-    def queries_of(g, tile):
-        return jnp.concatenate([q_rope[g, tile * tile_rows:(tile + 1) * tile_rows], units], axis=1)
-
-    far_blocks = range(0, REACH // 2)
-    near_blocks = range(REACH // 2, blocks)
-
-    def attend_near(g):
-        keys, values = operands(g, near_blocks)
-        for tile in range(tiles):
-            scores = jnp.dot(queries_of(g, tile), keys, preferred_element_type=jnp.float32)
-            top = jnp.max(scores, axis=1, keepdims=True)
-            weights = jnp.exp2((scores - top) * scale).astype(jnp.bfloat16)
-            sums[g, tile] = jnp.dot(weights, values, preferred_element_type=jnp.float32)
-            tops[g, tile] = jnp.broadcast_to(top, (tile_rows, HEAD_SIZE))
-
-    def attend_far(g):
-        keys, values = operands(g, far_blocks)
-        for tile in range(tiles):
-            scores = jnp.dot(queries_of(g, tile), keys, preferred_element_type=jnp.float32)
-            near_top = tops[g, tile]
-            top = jnp.maximum(near_top, jnp.max(scores, axis=1, keepdims=True))
-            wide = jnp.concatenate([top] * len(far_blocks), axis=1)
-            weights = jnp.exp2((scores - wide) * scale).astype(jnp.bfloat16)
-            factor = jnp.exp2((near_top - top) * scale)
-            mixed = jnp.dot(weights, values, preferred_element_type=jnp.float32)
-            mixed = sums[g, tile] * jnp.concatenate([factor, factor], axis=1) + mixed
-            mixed = mixed[:, :HEAD_SIZE] / mixed[:, HEAD_SIZE:]
-            for r in range(Q_TILE):
-                o_ref[g * copies + tile * Q_TILE + r] = mixed[r * rows:(r + 1) * rows].astype(jnp.bfloat16)
+    def near(g):
+        attend_near(win, hidden, q_rope, sums, tops, units, g)
+
+    def far(g):
+        attend_far(win, hidden, q_rope, sums, tops, units, g, o_ref, g * copies)
 
     arrivals = expected_arrivals([2 if kind == BOTH else 1 for kind, _ in order])
     last = groups - 1
@@ -363,7 +377,7 @@
         if g:
             relays(g)
         await_pieces(False, g)
-        attend_near(g)
+        near(g)
 
     @pl.loop(0, groups - AHEAD)
     def _(g):
@@ -377,7 +391,7 @@
         def _():
             from_peer(True, BOTH, jnp.maximum(g, 1), jnp.maximum(g, 1) + 1)
 
-        attend_far(g)
+        far(g)
         relays_in_loop(g, AHEAD + 1)
 
         @pl.when(g + AHEAD < last)
@@ -389,12 +403,13 @@
         def _():
             await_pieces(False, last)
 
-        attend_near(g + AHEAD)
+        near(g + AHEAD)
 
     for g in range(groups - AHEAD, groups):
         relays(reader["far", g])
         await_pieces(True, g)
-        attend_far(g)
+        if g < last:
+            far(g)
 
     whole = win.at[:, REACH]
     for kind, (condition, _, _, target) in plan.items():
@@ -406,10 +421,19 @@
             ).wait_send()
 
 
-def leave(heads_ref, o_hbm, sem):
-    for i in range(heads_ref.shape[0]):
+def leave(heads, win, hidden, q_rope, sums, tops, o_hbm, last_heads, sem):
+    done = heads.shape[0]
+
+    def put(source, i):
         at = pl.ds(i * HEAD_SIZE, HEAD_SIZE)
-        pltpu.make_async_copy(heads_ref.at[i], o_hbm.at[:, at], sem).start()
+        pltpu.make_async_copy(source, o_hbm.at[:, at], sem).start()
+
+    for i in range(done):
+        put(heads.at[i], i)
+    units = unit_rows(win.shape[3])
+    attend_far(win, hidden, q_rope, sums, tops, units, win.shape[0] - 1, last_heads, 0)
+    for i in range(last_heads.shape[0]):
+        put(last_heads.at[i], done + i)
     pltpu.make_async_copy(o_hbm, o_hbm, sem).wait()
 
 
@@ -426,19 +450,23 @@
         inv_freq = ROPE_BASE ** (-(np.arange(half_dim) * 2.0 / HEAD_SIZE))
         freq = jnp.asarray(np.concatenate([inv_freq, inv_freq])[None, :], jnp.float32)
         blocks = REACH + 1
-        heads = pl.pallas_call(
+        tiles, tile_rows = copies // Q_TILE, Q_TILE * rows
+        held = [
+            jax.ShapeDtypeStruct(((groups - 1) * copies, rows, HEAD_SIZE), jnp.bfloat16),
+            jax.ShapeDtypeStruct((groups, blocks, 2, rows, HEAD_SIZE), jnp.bfloat16),
+            jax.ShapeDtypeStruct((blocks, rows, rows), jnp.bfloat16),
+            jax.ShapeDtypeStruct((groups, copies * rows, HEAD_SIZE), jnp.bfloat16),
+            jax.ShapeDtypeStruct((groups, tiles, tile_rows, 2 * HEAD_SIZE), jnp.float32),
+            jax.ShapeDtypeStruct((groups, tiles, tile_rows, HEAD_SIZE), jnp.float32),
+        ]
+        state = pl.pallas_call(
             functools.partial(kernel, count, groups, copies, rows),
-            out_shape=jax.ShapeDtypeStruct((groups * copies, rows, HEAD_SIZE), jnp.bfloat16),
+            out_shape=held,
             in_specs=[pl.BlockSpec(memory_space=pl.ANY)] * 8,
-            out_specs=pl.BlockSpec(memory_space=pltpu.VMEM),
+            out_specs=[pl.BlockSpec(memory_space=pltpu.VMEM)] * len(held),
             scratch_shapes=[
-                pltpu.VMEM((groups, blocks, 2, rows, HEAD_SIZE), jnp.bfloat16),
-                pltpu.VMEM((blocks, rows, rows), jnp.bfloat16),
                 pltpu.VMEM((groups * copies, rows, HEAD_SIZE), jnp.bfloat16),
                 pltpu.VMEM(key_projection.shape, jnp.bfloat16),
-                pltpu.VMEM((groups, copies * rows, HEAD_SIZE), jnp.bfloat16),
-                pltpu.VMEM((groups, copies // Q_TILE, Q_TILE * rows, 2 * HEAD_SIZE), jnp.float32),
-                pltpu.VMEM((groups, copies // Q_TILE, Q_TILE * rows, HEAD_SIZE), jnp.float32),
                 pltpu.VMEM((1, HEAD_SIZE), jnp.float32),
                 pltpu.VMEM((1, HEAD_SIZE), jnp.float32),
                 pltpu.VMEM((1, HEAD_SIZE), jnp.float32),
@@ -451,7 +479,7 @@
                 pltpu.SemaphoreType.DMA((6, groups + 2)),
             ],
             compiler_params=pltpu.CompilerParams(
-                collective_id=0, has_side_effects=True, vmem_limit_bytes=41943040
+                collective_id=0, has_side_effects=True, vmem_limit_bytes=12 * 1024 * 1024
             ),
         )(
             *(pltpu.with_memory_space_constraint(array, pltpu.HBM) for array in (
@@ -462,11 +490,13 @@
         return pl.pallas_call(
             leave,
             out_shape=jax.ShapeDtypeStruct(query_proj.shape, jnp.bfloat16),
-            in_specs=[pl.BlockSpec(memory_space=pltpu.VMEM)],
+            in_specs=[pl.BlockSpec(memory_space=pltpu.VMEM)] * len(held),
             out_specs=pl.BlockSpec(memory_space=pl.ANY),
-            scratch_shapes=[pltpu.SemaphoreType.DMA],
+            scratch_shapes=[
+                pltpu.VMEM((copies, rows, HEAD_SIZE), jnp.bfloat16), pltpu.SemaphoreType.DMA,
+            ],
             compiler_params=pltpu.CompilerParams(vmem_limit_bytes=8 * 1024 * 1024),
-        )(heads)
+        )(*state)
 
     tokens = P(("dp", "sp"), None)
     vector = P(("dp", "sp"))

time: 35.3 us -> 35.1 us (level)
    pallas_call x1, Pallas kernels: 33.4 us -> 32.4 us  [body(): pl.pallas_call(functools.partial(kernel, count, groups, copies, rows), ou...]
    pallas_call x1, Pallas kernels: 1.29 us -> 2.09 us  [body(): pl.pallas_call(leave, out_shape=jax.ShapeDtypeStruct(query_proj.shape, jn...]
where the time goes in v7:
time: 35.1 us; the launch traced here: 34.5 us
  Pallas kernels  34.5 us (98%)
    pallas_call x1, Pallas kernels, body(): pl.pallas_call(functools.partial(kernel, count, groups, copies, rows), ou...  32.4 us
    pallas_call x1, Pallas kernels, body(): pl.pallas_call(leave, out_shape=jax.ShapeDtypeStruct(query_proj.shape, jn...  2.09 us

profile of v7, /device:TPU:16, one launch (start us, length us, event | category | flops | bytes accessed | tf_op | source)
XLA Modules:
  0.0 34.5 jit_solution(16870442371007055243)
XLA Ops:
  0.0 32.4 %shard_map.82 = (bf16[56,128,128]{2,1,0:T(8,128)(2,1)S(1)}, bf16[8,9,2,128,128]{4,3,2,1,0:T(8,128)(2,1)S(1)}, bf16[9,128,128]{2,1,0:T(8,128)(2,1)S(1)}, bf16[8,1...) custom-call(bf16[128,8192]{1,0:T(8,128)(2,1)} %q_hbm.1, ...), custom_call_target="tpu_custom_call" | custom-call | tf_op jit(solution)/shard_map/pallas_call | solution.py:462
  32.4 2.1 %shard_map.83 = bf16[128,8192]{1,0:T(8,128)(2,1)} custom-call(bf16[56,128,128]{2,1,0:T(8,128)(2,1)S(1)} %get-tuple-element.11.heads, bf16[8,9,2,128,128]{4,3,2,1,0:T(8,128)(2,1)S(1)} %get-tuple-element.12.win, bf16[9,128,128]{2,1,0:T(8,128)(2,1)S(1)} %get-tuple-element.13.hidden, bf16[8,1024,128]{2,1,0:T(8,128)(2,1)S(1)} %get-tuple-element.14.q_rope, ...), custom_call_target="tpu_custom_call" | custom-call | tf_op jit(solution)/shard_map/pallas_call | solution.py:490

commit v8 on v7

--- a/solution.py
+++ b/solution.py
@@ -17,9 +17,9 @@
 HIDDEN = -1e30
 Q_TILE = 1
 AHEAD = 2
-NEAR_TIME = 2.0
+NEAR_TIME = 1.8
 FAR_TIME = 1.5
-CORE_HOP = 1.6
+CORE_HOP = 1.4
 PATIENCE = 0.5
 EARLIER = 1
 MESH = pl.DeviceIdType.MESH
@@ -195,7 +195,7 @@
         for kind in (OWN_Z, OWN_Y, OWN_C):
             start(kind, n)
 
-    forwards = {4: (F4_Y, F4_C, F4_Z), 8: (F8_Y, F8_C), 2: (F2_C,), 6: (F6_C,)}
+    forwards = {4: (F4_C, F4_Z, F4_Y), 8: (F8_Y, F8_C), 2: (F2_C,), 6: (F6_C,)}
 
     def event(slot, n):
         @pl.when(me >= slot)

time: 35.1 us -> 35.1 us (level)
  no operation moved by 1% of the time
where the time goes in v8:
time: 35.1 us; the launch traced here: 34.5 us
  Pallas kernels  34.5 us (98%)
    pallas_call x1, Pallas kernels, body(): pl.pallas_call(functools.partial(kernel, count, groups, copies, rows), ou...  32.4 us
    pallas_call x1, Pallas kernels, body(): pl.pallas_call(leave, out_shape=jax.ShapeDtypeStruct(query_proj.shape, jn...  2.09 us

profile of v8, /device:TPU:16, one launch (start us, length us, event | category | flops | bytes accessed | tf_op | source)
XLA Modules:
  0.0 34.5 jit_solution(6964430735001974031)
XLA Ops:
  0.0 32.4 %shard_map.82 = (bf16[56,128,128]{2,1,0:T(8,128)(2,1)S(1)}, bf16[8,9,2,128,128]{4,3,2,1,0:T(8,128)(2,1)S(1)}, bf16[9,128,128]{2,1,0:T(8,128)(2,1)S(1)}, bf16[8,1...) custom-call(bf16[128,8192]{1,0:T(8,128)(2,1)} %q_hbm.1, ...), custom_call_target="tpu_custom_call" | custom-call | tf_op jit(solution)/shard_map/pallas_call | solution.py:462
  32.4 2.1 %shard_map.83 = bf16[128,8192]{1,0:T(8,128)(2,1)} custom-call(bf16[56,128,128]{2,1,0:T(8,128)(2,1)S(1)} %get-tuple-element.11.heads, bf16[8,9,2,128,128]{4,3,2,1,0:T(8,128)(2,1)S(1)} %get-tuple-element.12.win, bf16[9,128,128]{2,1,0:T(8,128)(2,1)S(1)} %get-tuple-element.13.hidden, bf16[8,1024,128]{2,1,0:T(8,128)(2,1)S(1)} %get-tuple-element.14.q_rope, ...), custom_call_target="tpu_custom_call" | custom-call | tf_op jit(solution)/shard_map/pallas_call | solution.py:490
